TPU v7x, 32 devices: a whole 2x2x4 slice. The times are simulated.
32 devices in a mesh: flow: 8 (over z, x), leaf: 4 (over y, core).
Axes of the slice: x: 2, y: 2, z: 4, core: 2. Of those that a mesh axis runs over, the one named last changes fastest.
Arguments:
- vel_coef: float32 [81, 16384], P(None, 'flow'), may hold values from -6 to 6
- gp_block: int32 [65536, 1], P(('flow', 'leaf')), may hold values from 0 to 7; in each aligned block of 2048 rows (0 to 2047, 2048 to 4095, ...) at most 512 rows name the same one
- gp_elem: int32 [65536], P(('flow', 'leaf')), may hold values from 0 to 2047
- gp_param: float32 [3, 65536], P(None, ('flow', 'leaf')), may hold values from 0 to 1
- gp_vel: float32 [3, 65536], P(None, ('flow', 'leaf')), may hold values from -6 to 6
- gp_weight: float32 [65536], P(('flow', 'leaf')), may hold values from 0.1 to 1
- gp_pos: float32 [3, 65536], P(None, ('flow', 'leaf')), may hold values from -4 to 4
- contact_patch: int32 [65536], P(('flow', 'leaf')), may hold values from 0 to 1023
- contact_param: float32 [2, 65536], P(None, ('flow', 'leaf')), may hold values from 0 to 1
- patch_ctrl: float32 [27, 8192], P(None, ('flow', 'leaf')), may hold values from -4 to 4
Outputs:
- flow_force: float32 [81, 16384], P(None, ('flow', 'leaf'))
- shell_force: float32 [3, 65536], P(None, ('flow', 'leaf'))
- patch_force: float32 [27, 8192], P(None, ('flow', 'leaf'))
Inputs may be any that keep to these rules, and one draw needn't show every extreme that they name: `gp_block`: the Gauss points of one device lie in at most 512 of each flow block's elements; some block is reached with exactly 512. `contact_patch`: A contact partner is one of the 1024 patches held by the Gauss point's own group, the devices of one index of flow.
All inputs are finite; a program needn't handle non-finite values.
Results may differ from a plain program's by a relative error of at most 0.0001.
Values sent between devices are 32-bit elements; how exact they have to be, the bound alone decides.
No kernel may reach another device: no remote copies, remote signals or barrier semaphores. Data moves between devices by JAX's collectives and lax.ppermute only.
A program may use at most 64 MiB of HBM per device.

v0:
```python
import functools

import jax
import jax.numpy as jnp
from jax import lax
from jax.experimental import pallas as pl
from jax.experimental.pallas import tpu as pltpu
from jax.sharding import PartitionSpec as P


BETA = 1.5
STIFF = 2.0
REACH = 0.5
VMEM_LIMIT = 20 * 2**20
GROUP = 512

F32, BF16, F8 = jnp.float32, jnp.bfloat16, jnp.float8_e4m3fn
I32, I16 = jnp.int32, jnp.int16
NN = (((1,), (0,)), ((), ()))
NT = (((1,), (1,)), ((), ()))


def dot(a, b, dims):
    return lax.dot_general(a, b, dims, preferred_element_type=F32)


def split(x):
    high = x.astype(BF16)
    low = (x - high.astype(F32)).astype(BF16)
    return jnp.concatenate([high, low], axis=0)


def rows_of(shape):
    return lax.broadcasted_iota(I32, shape, 0)


def one_hot(index, rows, offset=0):
    number = lax.broadcasted_iota(I16, (rows, index.shape[1]), 0)
    hit = number == (index - offset).astype(I16)
    return jnp.where(hit, jnp.asarray(1, BF16), jnp.asarray(0, BF16)).astype(F8)


def pick_basis(x, which):
    b0 = 0.5 * (1.0 - x) ** 2
    b1 = 0.5 * (1.0 + 2.0 * x - 2.0 * x * x)
    b2 = 0.5 * x * x
    return jnp.where(which == 0, b0, jnp.where(which == 1, b1, b2))


def solid_weights(x0, x1, x2):
    k = rows_of((32, 1))
    return pick_basis(x0, k // 9) * pick_basis(x1, (k // 3) % 3) * pick_basis(x2, k % 3)


def shell_weights(x0, x1):
    k = rows_of((16, 1))
    return pick_basis(x0, k // 3) * pick_basis(x1, k % 3)


def pack_kernel(block_ref, elem_ref, param_ref, vel_ref, weight_ref, out_ref, rank_ref, vals):
    owners, _, slots = out_ref.shape
    count = block_ref.shape[1]
    step = 256
    block = block_ref[...]
    mask = jnp.where(rows_of((owners, count)) == block, 1.0, 0.0)
    upto = (
        lax.broadcasted_iota(I32, (step, step), 0) <= lax.broadcasted_iota(I32, (step, step), 1)
    )
    upto = jnp.where(upto, 1.0, 0.0).astype(BF16)
    base = jnp.zeros((owners, 1), F32)
    ranks = []
    for i in range(count // step):
        part = mask[:, i * step : (i + 1) * step]
        running = dot(part.astype(BF16), upto, NN)
        ranks.append(jnp.sum(part * (running + (base - 1.0)), axis=0, keepdims=True))
        base = base + running[:, step - 1 : step]
    rank = jnp.concatenate(ranks, axis=1).astype(I32)
    rank_ref[...] = rank
    vals[0:1] = elem_ref[...].astype(F32) + 1.0
    vals[1:4] = param_ref[...]
    vals[4:7] = vel_ref[...]
    vals[7:8] = weight_ref[...]
    v = vals[...]
    terms = jnp.concatenate([v * mask[d : d + 1] for d in range(owners)], axis=0)
    packed = dot(split(terms), one_hot(rank, slots), NT)
    packed = packed[: owners * 8] + packed[owners * 8 :]
    for d in range(owners):
        out_ref[d] = packed[d * 8 : (d + 1) * 8]


def contact_kernel(me_ref, *refs, peers):
    ctrl_refs = refs[:peers]
    patch_ref, param_ref, pos_ref, coef_ref = refs[peers : peers + 4]
    push_ref, part_ref, table_ref, ctrl, tight, wide = refs[peers + 4 :]
    own = ctrl_refs[0].shape[1]
    me = me_ref[0]
    ctrl[...] = jnp.zeros_like(ctrl)
    for k in range(peers):
        for c in range(3):
            ctrl[c * 16 : c * 16 + 9, k * own : (k + 1) * own] = ctrl_refs[k][c * 9 : c * 9 + 9, :]
    patch = patch_ref[...]
    table = jnp.concatenate([one_hot(patch, own, (me ^ k) * own) for k in range(peers)], axis=0)
    picked = dot(split(ctrl[...]), table, NN)
    picked = picked[:48] + picked[48:]
    w = shell_weights(param_ref[0:1, :], param_ref[1:2, :])
    gaps = [
        pos_ref[c : c + 1, :] - jnp.sum(picked[c * 16 : c * 16 + 16] * w, axis=0, keepdims=True)
        for c in range(3)
    ]
    far = 1.0 + (gaps[0] * gaps[0] + gaps[1] * gaps[1] + gaps[2] * gaps[2]) / (REACH * REACH)
    pushes = [STIFF * g / far for g in gaps]
    for c in range(3):
        push_ref[c : c + 1, :] = pushes[c]
    terms = jnp.concatenate([-(w * f) for f in pushes], axis=0)
    part = dot(split(terms), table, NT)
    part = part[:48] + part[48:]
    for c in range(3):
        tight[c * 9 : c * 9 + 9] = part[c * 16 : c * 16 + 9]
    part_ref[...] = jnp.zeros_like(part_ref)
    for k in range(peers):
        part_ref[k, 0:14, 0:own] = tight[0:14, k * own : (k + 1) * own]
        part_ref[k, 0:13, own:] = tight[14:27, k * own : (k + 1) * own]
    wide[...] = jnp.zeros_like(wide)
    for c in range(3):
        wide[c * 32 : c * 32 + 27, :] = coef_ref[c * 27 : c * 27 + 27, :]
    table_ref[...] = split(wide[...])


def force_kernel(recv_ref, table_ref, part_ref, info_ref, beside_ref, across_ref):
    groups = recv_ref.shape[0]
    elements = table_ref.shape[1]
    for g in range(groups):
        point = recv_ref[g]
        index = point[0:1].astype(I32) - 1
        picked = dot(table_ref[...], one_hot(index, elements), NN)
        picked = picked[:96] + picked[96:]
        w = solid_weights(point[1:2], point[2:3], point[3:4])
        speed = [
            jnp.sum(picked[c * 32 : c * 32 + 32] * w, axis=0, keepdims=True) for c in range(3)
        ]
        scale = BETA * point[7:8]
        info_ref[g, 0:4] = point[0:4]
        for c in range(3):
            info_ref[g, 4 + c : 5 + c] = scale * (point[4 + c : 5 + c] - speed[c])
        info_ref[g, 7:8] = jnp.zeros((1, GROUP), F32)
        beside_ref[g * 8 : (g + 1) * 8] = info_ref[g]
        across_ref[g * 8 : (g + 1) * 8] = info_ref[g]
    tail = groups * 8
    beside_ref[tail:] = part_ref[1]
    across_ref[tail : tail + 16] = part_ref[2]
    across_ref[tail + 16 :] = part_ref[3]


def spread(source_ref, terms, first, rows):
    groups = terms.shape[1] // GROUP
    index = []
    for g in range(groups):
        point = source_ref[g * 8 : (g + 1) * 8]
        index.append(point[0:1].astype(I32))
        w = solid_weights(point[1:2], point[2:3], point[3:4])
        part = jnp.concatenate([w * point[4 + c : 5 + c] for c in range(3)], axis=0)
        terms[:, g * GROUP : (g + 1) * GROUP] = split(part)
    return dot(terms[...], one_hot(jnp.concatenate(index, axis=1), rows, first), NT)


def near_kernel(me_ref, own_ref, across_ref, part_ref, total_ref, patch_ref, terms):
    rows = total_ref.shape[1]
    tail = terms.shape[1] // GROUP * 8
    first = me_ref[0] * rows + 1
    total = spread(own_ref, terms, first, rows)
    total = total + spread(across_ref, terms, first, rows)
    total_ref[...] = total[:96] + total[96:]
    patch_ref[...] = part_ref[0] + across_ref[tail : tail + 16]


def last_kernel(me_ref, beside_ref, corner_ref, total_ref, part_ref, flow_ref, patch_ref, terms):
    rows = total_ref.shape[1]
    own = patch_ref.shape[1]
    tail = terms.shape[1] // GROUP * 8
    first = me_ref[0] * rows + 1
    total = spread(beside_ref, terms, first, rows)
    total = total + spread(corner_ref, terms, first, rows)
    total = total_ref[...] + total[:96] + total[96:]
    for c in range(3):
        flow_ref[c * 27 : c * 27 + 27, :] = total[c * 32 : c * 32 + 27]
    part = part_ref[...] + beside_ref[tail:] + corner_ref[tail + 16 :]
    patch_ref[0:14] = part[0:14, 0:own]
    patch_ref[14:27] = part[0:13, own:]


def finish_kernel(back_ref, block_ref, rank_ref, push_ref, out_ref):
    owners, _, slots = back_ref.shape
    back = back_ref[...].reshape(owners * 8, slots)
    got = dot(split(back), one_hot(rank_ref[...], slots), NN)
    got = got[: owners * 8] + got[owners * 8 :]
    block = block_ref[...]
    total = jnp.zeros((8, block.shape[1]), F32)
    for d in range(owners):
        total = total + jnp.where(block == d, got[d * 8 : (d + 1) * 8], 0.0)
    out_ref[...] = push_ref[...] - total[4:7]


def call(kernel, out_shape, scratch=(), smem=0, operands=(), flops=0, limit=VMEM_LIMIT):
    specs = [
        pl.BlockSpec(memory_space=pltpu.SMEM if i < smem else pltpu.VMEM)
        for i in range(len(operands))
    ]
    return pl.pallas_call(
        kernel,
        out_shape=out_shape,
        in_specs=specs,
        out_specs=jax.tree.map(lambda _: pl.BlockSpec(memory_space=pltpu.VMEM), out_shape),
        scratch_shapes=scratch,
        cost_estimate=pl.CostEstimate(flops=flops, bytes_accessed=0, transcendentals=0),
        compiler_params=pltpu.CompilerParams(vmem_limit_bytes=limit),
    )(*operands)


def shape(*dims, dtype=F32):
    return jax.ShapeDtypeStruct(dims, dtype)


def per_device(
    vel_coef, gp_block, gp_elem, gp_param, gp_vel, gp_weight, gp_pos, contact_patch,
    contact_param, patch_ctrl,
):
    owners = lax.axis_size("flow")
    peers = lax.axis_size("leaf")
    count = gp_elem.shape[0]
    slots = 2 * count // owners
    width = slots * owners
    groups = width // GROUP
    elements = vel_coef.shape[1]
    own = patch_ctrl.shape[1]
    me = lax.axis_index("leaf").astype(I32).reshape(1)

    def swap(x, k):
        return lax.ppermute(x, "leaf", [(i, i ^ k) for i in range(peers)])

    def to_groups(x):
        if slots == GROUP:
            return x
        return x.transpose(1, 0, 2).reshape(8, groups, GROUP).transpose(1, 0, 2)

    def to_owners(x):
        if slots == GROUP:
            return x
        return x.transpose(1, 0, 2).reshape(8, owners, slots).transpose(1, 0, 2)

    block = gp_block.reshape(1, count)
    far = swap(patch_ctrl, 2)
    payload, rank = call(
        pack_kernel,
        [shape(owners, 8, slots), shape(1, count, dtype=I32)],
        scratch=[pltpu.VMEM((8, count), F32)],
        operands=(block, gp_elem.reshape(1, count), gp_param, gp_vel, gp_weight.reshape(1, count)),
        flops=10**9,
        limit=None,
    )
    payload, far, here = lax.optimization_barrier((payload, far, patch_ctrl))
    ctrl = [here, swap(here, 1), far, swap(far, 1)]
    recv = lax.all_to_all(payload, "flow", split_axis=0, concat_axis=0, tiled=True)
    pushes, part, table = call(
        functools.partial(contact_kernel, peers=peers),
        [shape(3, count), shape(peers, 16, 2 * own), shape(192, elements, dtype=BF16)],
        scratch=[
            pltpu.VMEM((48, peers * own), F32),
            pltpu.VMEM((32, peers * own), F32),
            pltpu.VMEM((96, elements), F32),
        ],
        smem=1,
        operands=(me, *ctrl, contact_patch.reshape(1, count), contact_param, gp_pos, vel_coef),
        flops=10**9,
    )
    tail = groups * 8
    info, beside, across = call(
        force_kernel,
        [shape(groups, 8, GROUP), shape(tail + 16, GROUP), shape(tail + 32, GROUP)],
        operands=(to_groups(recv), table, part),
        flops=4 * 10**9,
    )
    from_across = swap(across, 2)
    back = lax.all_to_all(to_owners(info), "flow", split_axis=0, concat_axis=0, tiled=True)
    from_corner = swap(from_across, 1)
    from_beside = swap(beside, 1)
    rows = elements // peers
    total, patch_part = call(
        near_kernel,
        [shape(96, rows), shape(16, 2 * own)],
        scratch=[pltpu.VMEM((192, width), BF16)],
        smem=1,
        operands=(me, beside, from_across, part),
        flops=2 * 10**9,
    )
    flow_force, patch_force = call(
        last_kernel,
        [shape(81, rows), shape(27, own)],
        scratch=[pltpu.VMEM((192, width), BF16)],
        smem=1,
        operands=(me, from_beside, from_corner, total, patch_part),
        flops=2 * 10**9,
    )
    flow_force, pushes = lax.optimization_barrier((flow_force, pushes))
    shell_force = call(
        finish_kernel, shape(3, count),
        operands=(back, block, rank, pushes),
        flops=10**8,
    )
    return flow_force, shell_force, patch_force


def solution(mesh):
    both = ("flow", "leaf")
    in_specs = (
        P(None, "flow"), P(both, None), P(both), P(None, both), P(None, both), P(both),
        P(None, both), P(both), P(None, both), P(None, both),
    )
    out_specs = (P(None, both), P(None, both), P(None, both))

    return jax.shard_map(
        per_device, mesh=mesh, in_specs=in_specs, out_specs=out_specs, check_vma=False
    )
```

profile of v0, /device:TPU:0, one launch (start us, length us, event | category | flops | bytes accessed | tf_op | source)
XLA Modules:
  0.0 41.8 jit_solution(1532700607346956452)
XLA Ops:
  0.6 3.1 %collective-permute-start = (f32[27,256]{1,0:T(8,128)}, f32[27,256]{1,0:T(8,128)S(1)}, u32[]{:S(2)}, u32[]{:S(2)}) collective-permute-start(f32[27,256]{1,0:T(8,128)} %refs_0_), channel_id=1, source_target_pairs={{0,2},{1,3},{2,0},{3,1},{4,6},{5,7},{6,4},{7,5},{8,10},{9,11},{10,... | collective-permute-start | bytes 82952 | tf_op jit(solution)/shard_map/ppermute | solution.py:238
  3.7 2.2 %shard_map.121 = (f32[8,8,512]{2,1,0:T(8,128)}, s32[1,2048]{1,0:T(1,128)}) custom-call(s32[1,2048]{1,0:T(1,128)} %bitcast.6, s32[1,2048]{1,0:T(1,128)} %bitcast.8, f32[3,2048]{1,0:T(4,128)} %param_ref.1, f32[3,2048]{1,0:T(4,128)} %vel_ref.1, f32[1,2048]{1,0:T(1,128)} %bitcast.9), custom_call_target="tpu_custom_call" | custom-call | flops 1000000000 | tf_op jit(solution)/shard_map/pallas_call | solution.py:208
  5.9 0.0 copy-start.2
  5.9 0.0 copy-start.3
  5.9 6.3 %all-to-all-start = ((f32[8,8,512]{2,1,0:T(8,128)}), f32[8,8,512]{2,1,0:T(8,128)S(1)}, u32[]{:S(2)}, u32[]{:S(2)}) async-start(f32[8,8,512]{2,1,0:T(8,128)} %get-tuple-element.21), calls=%async_computation | async-start | bytes 262144 | tf_op jit(solution)/shard_map/all_to_all | solution.py:262
  12.2 0.0 copy-start.4
  12.3 0.1 collective-permute-start.1
  12.3 0.5 %collective-permute-start.2 = (f32[27,256]{1,0:T(8,128)S(1)}, f32[27,256]{1,0:T(8,128)S(1)}, u32[]{:S(2)}, u32[]{:S(2)}) collective-permute-start(f32[27,256]{1,0:T(8,128)S(1)} %collective-permute-done.refs_2_), channel_id=1, source_target_pairs={{0,1},{1,0},{2,3},{3,2},{4,5},{5,4},{6,7},{7,6},{8,9},{9,8},{10,11... | collective-permute-start | bytes 82952 | tf_op jit(solution)/shard_map/ppermute | solution.py:238
  12.8 0.7 %collective-permute-done.1.refs_1_ = f32[27,256]{1,0:T(8,128)S(1)} collective-permute-done((f32[27,256]{1,0:T(8,128)S(1)}, f32[27,256]{1,0:T(8,128)S(1)}, u32[]{:S(2)}, u32[]{:S(2)}) %collective-permute-start.1) | collective-permute-done | bytes 27680 | tf_op jit(solution)/shard_map/ppermute | solution.py:238
  13.5 0.2 collective-permute-done.2.refs_3_
  13.7 1.5 %shard_map.122 = (f32[3,2048]{1,0:T(4,128)S(1)}, f32[4,16,512]{2,1,0:T(8,128)S(1)}, bf16[192,2048]{1,0:T(8,128)(2,1)S(1)}) custom-call(s32[1]{0:T(128)} %bitcast.me_ref, f32[27,256]{1,0:T(8,128)S(1)} %copy-done.1, f32[27,256]{1,0:T(8,128)S(1)} %collective-permute-done.1.refs_1_, f32[27,256]{1,0:T(8,128)S(1)} %collective-permute-done.refs_2_, ...), custom_call_target="tpu_custom_call" | custom-call | flops 1000000000 | tf_op jit(solution)/shard_map/pallas_call | solution.py:208
  15.2 4.4 %all-to-all-done.recv_ref = f32[8,8,512]{2,1,0:T(8,128)S(1)} async-done(((f32[8,8,512]{2,1,0:T(8,128)}), f32[8,8,512]{2,1,0:T(8,128)S(1)}, u32[]{:S(2)}, u32[]{:S(2)}) %all-to-all-start) | async-done | bytes 131104 | tf_op jit(solution)/shard_map/all_to_all | solution.py:262
  19.6 4.2 %shard_map.123 = (f32[8,8,512]{2,1,0:T(8,128)}, f32[80,512]{1,0:T(8,128)S(1)}, f32[96,512]{1,0:T(8,128)S(1)}) custom-call(f32[8,8,512]{2,1,0:T(8,128)S(1)} %all-to-all-done.recv_ref, bf16[192,2048]{1,0:T(8,128)(2,1)S(1)} %get-tuple-element.24.table_ref, f32[4,16,512]{2,1,0:T(8,128)S(1)} %get-tuple-element.25.part_ref), custom_call_target="tpu_custom_call" | custom-call | flops 4000000000 | tf_op jit(solution)/shard_map/pallas_call | solution.py:208
  23.8 1.5 %collective-permute-start.4 = (f32[96,512]{1,0:T(8,128)S(1)}, f32[96,512]{1,0:T(8,128)S(1)}, u32[]{:S(2)}, u32[]{:S(2)}) collective-permute-start(f32[96,512]{1,0:T(8,128)S(1)} %get-tuple-element.27), channel_id=1, source_target_pairs={{0,2},{1,3},{2,0},{3,1},{4,6},{5,7},{6,4},{7,5},{8,10},{9,11},{10,... | collective-permute-start | bytes 589832 | tf_op jit(solution)/shard_map/ppermute | solution.py:238
  25.3 4.2 %collective-permute-done.4.across_ref = f32[96,512]{1,0:T(8,128)S(1)} collective-permute-done((f32[96,512]{1,0:T(8,128)S(1)}, f32[96,512]{1,0:T(8,128)S(1)}, u32[]{:S(2)}, u32[]{:S(2)}) %collective-permute-start.4) | collective-permute-done | bytes 196640 | tf_op jit(solution)/shard_map/ppermute | solution.py:238
  29.4 3.4 %all-to-all-start.1 = ((f32[8,8,512]{2,1,0:T(8,128)}), f32[8,8,512]{2,1,0:T(8,128)S(1)}, u32[]{:S(2)}, u32[]{:S(2)}) async-start(f32[8,8,512]{2,1,0:T(8,128)} %get-tuple-element.33), calls=%async_computation.1 | async-start | bytes 262144 | tf_op jit(solution)/shard_map/all_to_all | solution.py:283
  32.8 0.6 %collective-permute-start.3 = (f32[80,512]{1,0:T(8,128)S(1)}, f32[80,512]{1,0:T(8,128)S(1)}, u32[]{:S(2)}, u32[]{:S(2)}) collective-permute-start(f32[80,512]{1,0:T(8,128)S(1)} %get-tuple-element.26.own_ref), channel_id=1, source_target_pairs={{0,1},{1,0},{2,3},{3,2},{4,5},{5,4},{6,7},{7,6},{8,9},{9,8},{10,11... | collective-permute-start | bytes 491528 | tf_op jit(solution)/shard_map/ppermute | solution.py:238
  33.4 1.9 %shard_map.124 = (f32[96,512]{1,0:T(8,128)S(1)}, f32[16,512]{1,0:T(8,128)S(1)}) custom-call(s32[1]{0:T(128)} %bitcast.me_ref, f32[80,512]{1,0:T(8,128)S(1)} %get-tuple-element.26.own_ref, f32[96,512]{1,0:T(8,128)S(1)} %collective-permute-done.4.across_ref, f32[4,16,512]{2,1,0:T(8,128)S(1)} %get-tuple-element.25.part_ref), custom_call_target="tpu_custom_call" | custom-call | flops 2000000000 | tf_op jit(solution)/shard_map/pallas_call | solution.py:208
  35.3 0.0 collective-permute-done.5.corner_ref
  35.3 0.0 copy-start.5
  35.3 0.0 copy-start.6
  35.3 2.6 %shard_map.125 = (f32[81,512]{1,0:T(8,128)}, f32[27,256]{1,0:T(8,128)}) custom-call(s32[1]{0:T(128)} %bitcast.me_ref, f32[80,512]{1,0:T(8,128)S(1)} %collective-permute-done.3.beside_ref, f32[96,512]{1,0:T(8,128)S(1)} %collective-permute-done.5.corner_ref, f32[96,512]{1,0:T(8,128)S(1)} %get-tuple-element.28.total_ref, f32[16,512]{1,0:T(8,128)S(1)} %get-tuple-element.29.part_ref), custom_call_target="tpu_custom_call" | custom-call | flops 2000000000 | tf_op jit(solution)/shard_map/pallas_call | solution.py:208
  37.9 2.8 %all-to-all-done.1.back_ref = f32[8,8,512]{2,1,0:T(8,128)S(1)} async-done(((f32[8,8,512]{2,1,0:T(8,128)}), f32[8,8,512]{2,1,0:T(8,128)S(1)}, u32[]{:S(2)}, u32[]{:S(2)}) %all-to-all-start.1) | async-done | bytes 131104 | tf_op jit(solution)/shard_map/all_to_all | solution.py:283
  40.7 1.1 %shard_map.126 = f32[3,2048]{1,0:T(4,128)} custom-call(f32[8,8,512]{2,1,0:T(8,128)S(1)} %all-to-all-done.1.back_ref, s32[1,2048]{1,0:T(1,128)S(1)} %bitcast.7, s32[1,2048]{1,0:T(1,128)S(1)} %copy-done.6, f32[3,2048]{1,0:T(4,128)S(1)} %get-tuple-element.35.push_ref), custom_call_target="tpu_custom_call" | custom-call | flops 100000000 | tf_op jit(solution)/shard_map/pallas_call | solution.py:208
  (12 shorter events, 0.0 us)
Async XLA Ops:
  0.6 5.3 %collective-permute-start = (f32[27,256]{1,0:T(8,128)}, f32[27,256]{1,0:T(8,128)S(1)}, u32[]{:S(2)}, u32[]{:S(2)}) collective-permute-start(f32[27,256]{1,0:T(8,128)} %refs_0_), channel_id=1, source_target_pairs={{0,2},{1,3},{2,0},{3,1},{4,6},{5,7},{6,4},{7,5},{8,10},{9,11},{10,... | collective-permute-start | bytes 82952 | tf_op jit(solution)/shard_map/ppermute | solution.py:238
  3.7 10.0 %copy-start = (f32[81,2048]{1,0:T(8,128)S(1)}, f32[81,2048]{1,0:T(8,128)}, u32[]{:S(2)}) copy-start(f32[81,2048]{1,0:T(8,128)} %refs_7_.1) | copy-start | bytes 1990660
  5.9 6.3 %copy-start.1 = (f32[27,256]{1,0:T(8,128)S(1)}, f32[27,256]{1,0:T(8,128)}, u32[]{:S(2)}) copy-start(f32[27,256]{1,0:T(8,128)} %refs_0_) | copy-start | bytes 82948
  5.9 7.8 %copy-start.2 = (f32[3,2048]{1,0:T(4,128)S(1)}, f32[3,2048]{1,0:T(4,128)}, u32[]{:S(2)}) copy-start(f32[3,2048]{1,0:T(4,128)} %refs_6_.1) | copy-start | bytes 73732
  5.9 7.8 %copy-start.3 = (f32[2,2048]{1,0:T(2,128)S(1)}, f32[2,2048]{1,0:T(2,128)}, u32[]{:S(2)}) copy-start(f32[2,2048]{1,0:T(2,128)} %refs_5_.1) | copy-start | bytes 49156
  5.9 13.7 %all-to-all-start = ((f32[8,8,512]{2,1,0:T(8,128)}), f32[8,8,512]{2,1,0:T(8,128)S(1)}, u32[]{:S(2)}, u32[]{:S(2)}) async-start(f32[8,8,512]{2,1,0:T(8,128)} %get-tuple-element.21), calls=%async_computation | async-start | bytes 262144 | tf_op jit(solution)/shard_map/all_to_all | solution.py:262
  12.2 1.5 %copy-start.4 = (s32[2048]{0:T(1024)S(1)}, s32[2048]{0:T(1024)}, u32[]{:S(2)}) copy-start(s32[2048]{0:T(1024)} %param.17) | copy-start | bytes 24580
  12.3 1.3 %collective-permute-start.1 = (f32[27,256]{1,0:T(8,128)S(1)}, f32[27,256]{1,0:T(8,128)S(1)}, u32[]{:S(2)}, u32[]{:S(2)}) collective-permute-start(f32[27,256]{1,0:T(8,128)S(1)} %copy-done.1), channel_id=1, source_target_pairs={{0,1},{1,0},{2,3},{3,2},{4,5},{5,4},{6,7},{7,6},{8,9},{9,8},{10,11... | collective-permute-start | bytes 82952 | tf_op jit(solution)/shard_map/ppermute | solution.py:238
  12.3 1.4 %collective-permute-start.2 = (f32[27,256]{1,0:T(8,128)S(1)}, f32[27,256]{1,0:T(8,128)S(1)}, u32[]{:S(2)}, u32[]{:S(2)}) collective-permute-start(f32[27,256]{1,0:T(8,128)S(1)} %collective-permute-done.refs_2_), channel_id=1, source_target_pairs={{0,1},{1,0},{2,3},{3,2},{4,5},{5,4},{6,7},{7,6},{8,9},{9,8},{10,11... | collective-permute-start | bytes 82952 | tf_op jit(solution)/shard_map/ppermute | solution.py:238
  23.8 5.7 %collective-permute-start.4 = (f32[96,512]{1,0:T(8,128)S(1)}, f32[96,512]{1,0:T(8,128)S(1)}, u32[]{:S(2)}, u32[]{:S(2)}) collective-permute-start(f32[96,512]{1,0:T(8,128)S(1)} %get-tuple-element.27), channel_id=1, source_target_pairs={{0,2},{1,3},{2,0},{3,1},{4,6},{5,7},{6,4},{7,5},{8,10},{9,11},{10,... | collective-permute-start | bytes 589832 | tf_op jit(solution)/shard_map/ppermute | solution.py:238
  29.4 5.8 %collective-permute-start.5 = (f32[96,512]{1,0:T(8,128)S(1)}, f32[96,512]{1,0:T(8,128)S(1)}, u32[]{:S(2)}, u32[]{:S(2)}) collective-permute-start(f32[96,512]{1,0:T(8,128)S(1)} %collective-permute-done.4.across_ref), channel_id=1, source_target_pairs={{0,1},{1,0},{2,3},{3,2},{4,5},{5,4},{6,7},{7,6},{8,9},{9,8},{10,11... | collective-permute-start | bytes 589832 | tf_op jit(solution)/shard_map/ppermute | solution.py:238
  29.4 11.2 %all-to-all-start.1 = ((f32[8,8,512]{2,1,0:T(8,128)}), f32[8,8,512]{2,1,0:T(8,128)S(1)}, u32[]{:S(2)}, u32[]{:S(2)}) async-start(f32[8,8,512]{2,1,0:T(8,128)} %get-tuple-element.33), calls=%async_computation.1 | async-start | bytes 262144 | tf_op jit(solution)/shard_map/all_to_all | solution.py:283
  32.8 2.4 %collective-permute-start.3 = (f32[80,512]{1,0:T(8,128)S(1)}, f32[80,512]{1,0:T(8,128)S(1)}, u32[]{:S(2)}, u32[]{:S(2)}) collective-permute-start(f32[80,512]{1,0:T(8,128)S(1)} %get-tuple-element.26.own_ref), channel_id=1, source_target_pairs={{0,1},{1,0},{2,3},{3,2},{4,5},{5,4},{6,7},{7,6},{8,9},{9,8},{10,11... | collective-permute-start | bytes 491528 | tf_op jit(solution)/shard_map/ppermute | solution.py:238
  35.3 5.4 %copy-start.5 = (s32[2048,1]{0,1:T(1,128)S(1)}, s32[2048,1]{0,1:T(1,128)}, u32[]{:S(2)}) copy-start(s32[2048,1]{0,1:T(1,128)} %param.11) | copy-start | bytes 24580
  35.3 5.4 %copy-start.6 = (s32[1,2048]{1,0:T(1,128)S(1)}, s32[1,2048]{1,0:T(1,128)}, u32[]{:S(2)}) copy-start(s32[1,2048]{1,0:T(1,128)} %get-tuple-element.34.rank_ref) | copy-start | bytes 24580
where the time goes:
time: 42.2 us; the launch traced here: 41.8 us
  starting transfers between devices  15.4 us (36%)
  Pallas kernels  13.3 us (32%)
  waiting for transfers between devices  12.2 us (29%)
  between operations  0.74 us (2%)
    pallas_call x6, Pallas kernels, call(): pl.pallas_call(kernel, out_shape=out_shape, in_specs=specs, out_specs=jax...  13.3 us
    all_to_all x1, starting transfers between devices, per_device(): lax.all_to_all(payload, 'flow', split_axis=0, concat_axis=0, tiled=True)  6.31 us
    ppermute x6, starting transfers between devices, swap(): return lax.ppermute(x, 'leaf', [(i, i ^ k) for i in range(peers)])  5.72 us
    ppermute x6, waiting for transfers between devices, swap(): return lax.ppermute(x, 'leaf', [(i, i ^ k) for i in range(peers)])  5.02 us
    all_to_all x1, waiting for transfers between devices, per_device(): lax.all_to_all(payload, 'flow', split_axis=0, concat_axis=0, tiled=True)  4.4 us
    all_to_all x1, starting transfers between devices, per_device(): lax.all_to_all(to_owners(info), 'flow', split_axis=0, concat_axis=0, tile...  3.37 us
    all_to_all x1, waiting for transfers between devices, per_device(): lax.all_to_all(to_owners(info), 'flow', split_axis=0, concat_axis=0, tile...  2.82 us
  transfers between devices with their start and end apart: 8, of which 5 were waited for; matrix products, arithmetic and copies ran while one was open for 0% of the time, Pallas kernels for 19%

commit v1 on v0

--- a/solution.py
+++ b/solution.py
@@ -126,7 +126,7 @@
     table_ref[...] = split(wide[...])
 
 
-def force_kernel(recv_ref, table_ref, part_ref, info_ref, beside_ref, across_ref):
+def force_kernel(recv_ref, table_ref, part_ref, back_ref, beside_ref, across_ref):
     groups = recv_ref.shape[0]
     elements = table_ref.shape[1]
     for g in range(groups):
@@ -139,12 +139,14 @@
             jnp.sum(picked[c * 32 : c * 32 + 32] * w, axis=0, keepdims=True) for c in range(3)
         ]
         scale = BETA * point[7:8]
-        info_ref[g, 0:4] = point[0:4]
+        beside_ref[g * 8 : g * 8 + 4] = point[0:4]
         for c in range(3):
-            info_ref[g, 4 + c : 5 + c] = scale * (point[4 + c : 5 + c] - speed[c])
-        info_ref[g, 7:8] = jnp.zeros((1, GROUP), F32)
-        beside_ref[g * 8 : (g + 1) * 8] = info_ref[g]
-        across_ref[g * 8 : (g + 1) * 8] = info_ref[g]
+            force = scale * (point[4 + c : 5 + c] - speed[c])
+            beside_ref[g * 8 + 4 + c : g * 8 + 5 + c] = force
+            back_ref[g, c : c + 1] = force
+        beside_ref[g * 8 + 7 : g * 8 + 8] = jnp.zeros((1, GROUP), F32)
+        back_ref[g, 3:4] = jnp.zeros((1, GROUP), F32)
+        across_ref[g * 8 : (g + 1) * 8] = beside_ref[g * 8 : (g + 1) * 8]
     tail = groups * 8
     beside_ref[tail:] = part_ref[1]
     across_ref[tail : tail + 16] = part_ref[2]
@@ -188,16 +190,18 @@
     patch_ref[14:27] = part[0:13, own:]
 
 
-def finish_kernel(back_ref, block_ref, rank_ref, push_ref, out_ref):
+def finish_kernel(back_ref, block_ref, rank_ref, push_ref, out_ref, rows):
     owners, _, slots = back_ref.shape
-    back = back_ref[...].reshape(owners * 8, slots)
-    got = dot(split(back), one_hot(rank_ref[...], slots), NN)
-    got = got[: owners * 8] + got[owners * 8 :]
+    for d in range(owners):
+        rows[d * 4 : (d + 1) * 4] = back_ref[d]
+    got = dot(split(rows[...]), one_hot(rank_ref[...], slots), NN)
+    got = got[: owners * 4] + got[owners * 4 :]
     block = block_ref[...]
+    half = rows_of((8, 1)) // 4
     total = jnp.zeros((8, block.shape[1]), F32)
-    for d in range(owners):
-        total = total + jnp.where(block == d, got[d * 8 : (d + 1) * 8], 0.0)
-    out_ref[...] = push_ref[...] - total[4:7]
+    for d in range(owners // 2):
+        total = total + jnp.where(block - half == 2 * d, got[d * 8 : (d + 1) * 8], 0.0)
+    out_ref[...] = push_ref[...] - (total[0:3] + total[4:7])
 
 
 def call(kernel, out_shape, scratch=(), smem=0, operands=(), flops=0, limit=VMEM_LIMIT):
@@ -240,15 +244,14 @@
     def to_groups(x):
         if slots == GROUP:
             return x
-        return x.transpose(1, 0, 2).reshape(8, groups, GROUP).transpose(1, 0, 2)
+        return x.transpose(1, 0, 2).reshape(-1, groups, GROUP).transpose(1, 0, 2)
 
     def to_owners(x):
         if slots == GROUP:
             return x
-        return x.transpose(1, 0, 2).reshape(8, owners, slots).transpose(1, 0, 2)
+        return x.transpose(1, 0, 2).reshape(-1, owners, slots).transpose(1, 0, 2)
 
     block = gp_block.reshape(1, count)
-    far = swap(patch_ctrl, 2)
     payload, rank = call(
         pack_kernel,
         [shape(owners, 8, slots), shape(1, count, dtype=I32)],
@@ -257,9 +260,12 @@
         flops=10**9,
         limit=None,
     )
-    payload, far, here = lax.optimization_barrier((payload, far, patch_ctrl))
-    ctrl = [here, swap(here, 1), far, swap(far, 1)]
+    payload, here = lax.optimization_barrier((payload, patch_ctrl))
+    far = swap(here, 2)
     recv = lax.all_to_all(payload, "flow", split_axis=0, concat_axis=0, tiled=True)
+    twin = swap(here, 1)
+    diag = swap(far, 1)
+    ctrl = (here, twin, far, diag)
     pushes, part, table = call(
         functools.partial(contact_kernel, peers=peers),
         [shape(3, count), shape(peers, 16, 2 * own), shape(192, elements, dtype=BF16)],
@@ -273,14 +279,14 @@
         flops=10**9,
     )
     tail = groups * 8
-    info, beside, across = call(
+    force, beside, across = call(
         force_kernel,
-        [shape(groups, 8, GROUP), shape(tail + 16, GROUP), shape(tail + 32, GROUP)],
+        [shape(groups, 4, GROUP), shape(tail + 16, GROUP), shape(tail + 32, GROUP)],
         operands=(to_groups(recv), table, part),
         flops=4 * 10**9,
     )
     from_across = swap(across, 2)
-    back = lax.all_to_all(to_owners(info), "flow", split_axis=0, concat_axis=0, tiled=True)
+    back = lax.all_to_all(to_owners(force), "flow", split_axis=0, concat_axis=0, tiled=True)
     from_corner = swap(from_across, 1)
     from_beside = swap(beside, 1)
     rows = elements // peers
@@ -303,6 +309,7 @@
     flow_force, pushes = lax.optimization_barrier((flow_force, pushes))
     shell_force = call(
         finish_kernel, shape(3, count),
+        scratch=[pltpu.VMEM((owners * 4, slots), F32)],
         operands=(back, block, rank, pushes),
         flops=10**8,
     )

time: 42.2 us -> 42.4 us (level)
  starting transfers between devices: 15.4 us -> 16.8 us
  waiting for transfers between devices: 12.2 us -> 11.3 us
    all_to_all x1, waiting for transfers between devices: 4.4 us -> 0.65 us  [per_device(): lax.all_to_all(payload, 'flow', split_axis=0, concat_axis=0, tiled=True)]
    ppermute x6, waiting for transfers between devices: 5.02 us -> 8.41 us  [swap(): return lax.ppermute(x, 'leaf', [(i, i ^ k) for i in range(peers)])]
    all_to_all x1, starting transfers between devices: 3.37 us -> 5.98 us  [per_device(): lax.all_to_all(to_owners(force), 'flow', split_axis=0, concat_axis=0, til...]
    ppermute x6, starting transfers between devices: 5.72 us -> 3.34 us  [swap(): return lax.ppermute(x, 'leaf', [(i, i ^ k) for i in range(peers)])]
    all_to_all x1, starting transfers between devices: 6.31 us -> 7.43 us  [per_device(): lax.all_to_all(payload, 'flow', split_axis=0, concat_axis=0, tiled=True)]
    all_to_all x1, waiting for transfers between devices: 2.82 us -> 2.2 us  [per_device(): lax.all_to_all(to_owners(force), 'flow', split_axis=0, concat_axis=0, til...]
  transfers between devices with their start and end apart: 8 -> 8, of which waited for: 5 -> 5; matrix products, arithmetic and copies ran while one was open for 0% -> 0% of each run, Pallas kernels for 19% -> 14%
where the time goes in v1:
time: 42.4 us; the launch traced here: 42 us
  starting transfers between devices  16.8 us (40%)
  Pallas kernels  13.2 us (31%)
  waiting for transfers between devices  11.3 us (27%)
  between operations  0.73 us (2%)
    pallas_call x6, Pallas kernels, call(): pl.pallas_call(kernel, out_shape=out_shape, in_specs=specs, out_specs=jax...  13.2 us
    ppermute x6, waiting for transfers between devices, swap(): return lax.ppermute(x, 'leaf', [(i, i ^ k) for i in range(peers)])  8.41 us
    all_to_all x1, starting transfers between devices, per_device(): lax.all_to_all(payload, 'flow', split_axis=0, concat_axis=0, tiled=True)  7.43 us
    all_to_all x1, starting transfers between devices, per_device(): lax.all_to_all(to_owners(force), 'flow', split_axis=0, concat_axis=0, til...  5.98 us
    ppermute x6, starting transfers between devices, swap(): return lax.ppermute(x, 'leaf', [(i, i ^ k) for i in range(peers)])  3.34 us
    all_to_all x1, waiting for transfers between devices, per_device(): lax.all_to_all(to_owners(force), 'flow', split_axis=0, concat_axis=0, til...  2.2 us
  transfers between devices with their start and end apart: 8, of which 5 were waited for; matrix products, arithmetic and copies ran while one was open for 0% of the time, Pallas kernels for 14%

profile of v1, /device:TPU:0, one launch (start us, length us, event | category | flops | bytes accessed | tf_op | source)
XLA Modules:
  0.0 42.0 jit_solution(17711360668738137181)
XLA Ops:
  0.6 2.2 %shard_map.121 = (f32[8,8,512]{2,1,0:T(8,128)}, s32[1,2048]{1,0:T(1,128)}) custom-call(s32[1,2048]{1,0:T(1,128)} %bitcast.6, s32[1,2048]{1,0:T(1,128)} %bitcast.8, f32[3,2048]{1,0:T(4,128)} %param_ref.1, f32[3,2048]{1,0:T(4,128)} %vel_ref.1, f32[1,2048]{1,0:T(1,128)} %bitcast.9), custom_call_target="tpu_custom_call" | custom-call | flops 1000000000 | tf_op jit(solution)/shard_map/pallas_call | solution.py:212
  2.9 7.4 %all-to-all-start = ((f32[8,8,512]{2,1,0:T(8,128)}), f32[8,8,512]{2,1,0:T(8,128)S(1)}, u32[]{:S(2)}, u32[]{:S(2)}) async-start(f32[8,8,512]{2,1,0:T(8,128)} %get-tuple-element.20), calls=%async_computation | async-start | bytes 262144 | tf_op jit(solution)/shard_map/all_to_all | solution.py:265
  10.3 0.0 copy-start.4
  10.3 1.6 %collective-permute-start.1 = (f32[27,256]{1,0:T(8,128)S(1)}, f32[27,256]{1,0:T(8,128)S(1)}, u32[]{:S(2)}, u32[]{:S(2)}) collective-permute-start(f32[27,256]{1,0:T(8,128)S(1)} %copy-done.1), channel_id=1, source_target_pairs={{0,2},{1,3},{2,0},{3,1},{4,6},{5,7},{6,4},{7,5},{8,10},{9,11},{10,... | collective-permute-start | bytes 82952 | tf_op jit(solution)/shard_map/ppermute | solution.py:242
  11.9 0.0 collective-permute-start
  11.9 2.4 %collective-permute-done.1.refs_2_ = f32[27,256]{1,0:T(8,128)S(1)} collective-permute-done((f32[27,256]{1,0:T(8,128)S(1)}, f32[27,256]{1,0:T(8,128)S(1)}, u32[]{:S(2)}, u32[]{:S(2)}) %collective-permute-start.1) | collective-permute-done | bytes 27680 | tf_op jit(solution)/shard_map/ppermute | solution.py:242
  14.3 0.0 collective-permute-start.2
  14.3 0.0 collective-permute-done.refs_1_
  14.3 1.2 %collective-permute-done.2.refs_3_ = f32[27,256]{1,0:T(8,128)S(1)} collective-permute-done((f32[27,256]{1,0:T(8,128)S(1)}, f32[27,256]{1,0:T(8,128)S(1)}, u32[]{:S(2)}, u32[]{:S(2)}) %collective-permute-start.2) | collective-permute-done | bytes 27680 | tf_op jit(solution)/shard_map/ppermute | solution.py:242
  15.5 1.5 %shard_map.122 = (f32[3,2048]{1,0:T(4,128)S(1)}, f32[4,16,512]{2,1,0:T(8,128)S(1)}, bf16[192,2048]{1,0:T(8,128)(2,1)S(1)}) custom-call(s32[1]{0:T(128)} %bitcast.me_ref, f32[27,256]{1,0:T(8,128)S(1)} %copy-done.1, f32[27,256]{1,0:T(8,128)S(1)} %collective-permute-done.refs_1_, f32[27,256]{1,0:T(8,128)S(1)} %collective-permute-done.1.refs_2_, ...), custom_call_target="tpu_custom_call" | custom-call | flops 1000000000 | tf_op jit(solution)/shard_map/pallas_call | solution.py:212
  17.0 0.6 %all-to-all-done.recv_ref = f32[8,8,512]{2,1,0:T(8,128)S(1)} async-done(((f32[8,8,512]{2,1,0:T(8,128)}), f32[8,8,512]{2,1,0:T(8,128)S(1)}, u32[]{:S(2)}, u32[]{:S(2)}) %all-to-all-start) | async-done | bytes 131104 | tf_op jit(solution)/shard_map/all_to_all | solution.py:265
  17.6 4.2 %shard_map.123 = (f32[8,4,512]{2,1,0:T(4,128)}, f32[80,512]{1,0:T(8,128)S(1)}, f32[96,512]{1,0:T(8,128)S(1)}) custom-call(f32[8,8,512]{2,1,0:T(8,128)S(1)} %all-to-all-done.recv_ref, bf16[192,2048]{1,0:T(8,128)(2,1)S(1)} %get-tuple-element.22.table_ref, f32[4,16,512]{2,1,0:T(8,128)S(1)} %get-tuple-element.23.part_ref), custom_call_target="tpu_custom_call" | custom-call | flops 4000000000 | tf_op jit(solution)/shard_map/pallas_call | solution.py:212
  21.8 1.5 %collective-permute-start.4 = (f32[96,512]{1,0:T(8,128)S(1)}, f32[96,512]{1,0:T(8,128)S(1)}, u32[]{:S(2)}, u32[]{:S(2)}) collective-permute-start(f32[96,512]{1,0:T(8,128)S(1)} %get-tuple-element.25), channel_id=1, source_target_pairs={{0,2},{1,3},{2,0},{3,1},{4,6},{5,7},{6,4},{7,5},{8,10},{9,11},{10,... | collective-permute-start | bytes 589832 | tf_op jit(solution)/shard_map/ppermute | solution.py:242
  23.3 4.8 %collective-permute-done.4.across_ref = f32[96,512]{1,0:T(8,128)S(1)} collective-permute-done((f32[96,512]{1,0:T(8,128)S(1)}, f32[96,512]{1,0:T(8,128)S(1)}, u32[]{:S(2)}, u32[]{:S(2)}) %collective-permute-start.4) | collective-permute-done | bytes 196640 | tf_op jit(solution)/shard_map/ppermute | solution.py:242
  28.1 0.0 collective-permute-start.5
  28.1 6.0 %all-to-all-start.1 = ((f32[8,4,512]{2,1,0:T(4,128)}), f32[8,4,512]{2,1,0:T(4,128)S(1)}, u32[]{:S(2)}, u32[]{:S(2)}) async-start(f32[8,4,512]{2,1,0:T(4,128)} %get-tuple-element.31), calls=%async_computation.1 | async-start | bytes 131072 | tf_op jit(solution)/shard_map/all_to_all | solution.py:289
  34.1 0.2 collective-permute-start.3
  34.3 1.9 %shard_map.124 = (f32[96,512]{1,0:T(8,128)S(1)}, f32[16,512]{1,0:T(8,128)S(1)}) custom-call(s32[1]{0:T(128)} %bitcast.me_ref, f32[80,512]{1,0:T(8,128)S(1)} %get-tuple-element.24.own_ref, f32[96,512]{1,0:T(8,128)S(1)} %collective-permute-done.4.across_ref, f32[4,16,512]{2,1,0:T(8,128)S(1)} %get-tuple-element.23.part_ref), custom_call_target="tpu_custom_call" | custom-call | flops 2000000000 | tf_op jit(solution)/shard_map/pallas_call | solution.py:212
  36.2 0.0 collective-permute-done.5.corner_ref
  36.2 0.0 copy-start.5
  36.2 0.0 copy-start.6
  36.3 2.6 %shard_map.125 = (f32[81,512]{1,0:T(8,128)}, f32[27,256]{1,0:T(8,128)}) custom-call(s32[1]{0:T(128)} %bitcast.me_ref, f32[80,512]{1,0:T(8,128)S(1)} %collective-permute-done.3.beside_ref, f32[96,512]{1,0:T(8,128)S(1)} %collective-permute-done.5.corner_ref, f32[96,512]{1,0:T(8,128)S(1)} %get-tuple-element.26.total_ref, f32[16,512]{1,0:T(8,128)S(1)} %get-tuple-element.27.part_ref), custom_call_target="tpu_custom_call" | custom-call | flops 2000000000 | tf_op jit(solution)/shard_map/pallas_call | solution.py:212
  38.8 2.2 %all-to-all-done.1.back_ref = f32[8,4,512]{2,1,0:T(4,128)S(1)} async-done(((f32[8,4,512]{2,1,0:T(4,128)}), f32[8,4,512]{2,1,0:T(4,128)S(1)}, u32[]{:S(2)}, u32[]{:S(2)}) %all-to-all-start.1) | async-done | bytes 65568 | tf_op jit(solution)/shard_map/all_to_all | solution.py:289
  41.0 1.0 %shard_map.126 = f32[3,2048]{1,0:T(4,128)} custom-call(f32[8,4,512]{2,1,0:T(4,128)S(1)} %all-to-all-done.1.back_ref, s32[1,2048]{1,0:T(1,128)S(1)} %bitcast.7, s32[1,2048]{1,0:T(1,128)S(1)} %copy-done.6, f32[3,2048]{1,0:T(4,128)S(1)} %get-tuple-element.33.push_ref), custom_call_target="tpu_custom_call" | custom-call | flops 100000000 | tf_op jit(solution)/shard_map/pallas_call | solution.py:212
  (12 shorter events, 0.0 us)
Async XLA Ops:
  0.6 14.9 %copy-start = (f32[81,2048]{1,0:T(8,128)S(1)}, f32[81,2048]{1,0:T(8,128)}, u32[]{:S(2)}) copy-start(f32[81,2048]{1,0:T(8,128)} %refs_7_.1) | copy-start | bytes 1990660
  2.8 7.4 %copy-start.1 = (f32[27,256]{1,0:T(8,128)S(1)}, f32[27,256]{1,0:T(8,128)}, u32[]{:S(2)}) copy-start(f32[27,256]{1,0:T(8,128)} %refs_0_) | copy-start | bytes 82948
  2.8 12.7 %copy-start.2 = (f32[3,2048]{1,0:T(4,128)S(1)}, f32[3,2048]{1,0:T(4,128)}, u32[]{:S(2)}) copy-start(f32[3,2048]{1,0:T(4,128)} %refs_6_.1) | copy-start | bytes 73732
  2.8 12.7 %copy-start.3 = (f32[2,2048]{1,0:T(2,128)S(1)}, f32[2,2048]{1,0:T(2,128)}, u32[]{:S(2)}) copy-start(f32[2,2048]{1,0:T(2,128)} %refs_5_.1) | copy-start | bytes 49156
  2.9 14.8 %all-to-all-start = ((f32[8,8,512]{2,1,0:T(8,128)}), f32[8,8,512]{2,1,0:T(8,128)S(1)}, u32[]{:S(2)}, u32[]{:S(2)}) async-start(f32[8,8,512]{2,1,0:T(8,128)} %get-tuple-element.20), calls=%async_computation | async-start | bytes 262144 | tf_op jit(solution)/shard_map/all_to_all | solution.py:265
  10.3 5.2 %copy-start.4 = (s32[2048]{0:T(1024)S(1)}, s32[2048]{0:T(1024)}, u32[]{:S(2)}) copy-start(s32[2048]{0:T(1024)} %param.17) | copy-start | bytes 24580
  10.3 4.0 %collective-permute-start.1 = (f32[27,256]{1,0:T(8,128)S(1)}, f32[27,256]{1,0:T(8,128)S(1)}, u32[]{:S(2)}, u32[]{:S(2)}) collective-permute-start(f32[27,256]{1,0:T(8,128)S(1)} %copy-done.1), channel_id=1, source_target_pairs={{0,2},{1,3},{2,0},{3,1},{4,6},{5,7},{6,4},{7,5},{8,10},{9,11},{10,... | collective-permute-start | bytes 82952 | tf_op jit(solution)/shard_map/ppermute | solution.py:242
  11.9 2.4 %collective-permute-start = (f32[27,256]{1,0:T(8,128)S(1)}, f32[27,256]{1,0:T(8,128)S(1)}, u32[]{:S(2)}, u32[]{:S(2)}) collective-permute-start(f32[27,256]{1,0:T(8,128)S(1)} %copy-done.1), channel_id=1, source_target_pairs={{0,1},{1,0},{2,3},{3,2},{4,5},{5,4},{6,7},{7,6},{8,9},{9,8},{10,11... | collective-permute-start | bytes 82952 | tf_op jit(solution)/shard_map/ppermute | solution.py:242
  14.3 1.2 %collective-permute-start.2 = (f32[27,256]{1,0:T(8,128)S(1)}, f32[27,256]{1,0:T(8,128)S(1)}, u32[]{:S(2)}, u32[]{:S(2)}) collective-permute-start(f32[27,256]{1,0:T(8,128)S(1)} %collective-permute-done.1.refs_2_), channel_id=1, source_target_pairs={{0,1},{1,0},{2,3},{3,2},{4,5},{5,4},{6,7},{7,6},{8,9},{9,8},{10,11... | collective-permute-start | bytes 82952 | tf_op jit(solution)/shard_map/ppermute | solution.py:242
  21.8 6.3 %collective-permute-start.4 = (f32[96,512]{1,0:T(8,128)S(1)}, f32[96,512]{1,0:T(8,128)S(1)}, u32[]{:S(2)}, u32[]{:S(2)}) collective-permute-start(f32[96,512]{1,0:T(8,128)S(1)} %get-tuple-element.25), channel_id=1, source_target_pairs={{0,2},{1,3},{2,0},{3,1},{4,6},{5,7},{6,4},{7,5},{8,10},{9,11},{10,... | collective-permute-start | bytes 589832 | tf_op jit(solution)/shard_map/ppermute | solution.py:242
  28.1 8.1 %collective-permute-start.5 = (f32[96,512]{1,0:T(8,128)S(1)}, f32[96,512]{1,0:T(8,128)S(1)}, u32[]{:S(2)}, u32[]{:S(2)}) collective-permute-start(f32[96,512]{1,0:T(8,128)S(1)} %collective-permute-done.4.across_ref), channel_id=1, source_target_pairs={{0,1},{1,0},{2,3},{3,2},{4,5},{5,4},{6,7},{7,6},{8,9},{9,8},{10,11... | collective-permute-start | bytes 589832 | tf_op jit(solution)/shard_map/ppermute | solution.py:242
  28.1 12.9 %all-to-all-start.1 = ((f32[8,4,512]{2,1,0:T(4,128)}), f32[8,4,512]{2,1,0:T(4,128)S(1)}, u32[]{:S(2)}, u32[]{:S(2)}) async-start(f32[8,4,512]{2,1,0:T(4,128)} %get-tuple-element.31), calls=%async_computation.1 | async-start | bytes 131072 | tf_op jit(solution)/shard_map/all_to_all | solution.py:289
  34.1 2.1 %collective-permute-start.3 = (f32[80,512]{1,0:T(8,128)S(1)}, f32[80,512]{1,0:T(8,128)S(1)}, u32[]{:S(2)}, u32[]{:S(2)}) collective-permute-start(f32[80,512]{1,0:T(8,128)S(1)} %get-tuple-element.24.own_ref), channel_id=1, source_target_pairs={{0,1},{1,0},{2,3},{3,2},{4,5},{5,4},{6,7},{7,6},{8,9},{9,8},{10,11... | collective-permute-start | bytes 491528 | tf_op jit(solution)/shard_map/ppermute | solution.py:242
  36.2 4.8 %copy-start.5 = (s32[2048,1]{0,1:T(1,128)S(1)}, s32[2048,1]{0,1:T(1,128)}, u32[]{:S(2)}) copy-start(s32[2048,1]{0,1:T(1,128)} %param.11) | copy-start | bytes 24580
  36.2 4.8 %copy-start.6 = (s32[1,2048]{1,0:T(1,128)S(1)}, s32[1,2048]{1,0:T(1,128)}, u32[]{:S(2)}) copy-start(s32[1,2048]{1,0:T(1,128)} %get-tuple-element.32.rank_ref) | copy-start | bytes 24580

commit v2 on v1

--- a/solution.py
+++ b/solution.py
@@ -47,9 +47,27 @@
     return jnp.where(which == 0, b0, jnp.where(which == 1, b1, b2))
 
 
+def split_solid(x):
+    high = x[:80].astype(BF16)
+    low = (x[:80] - high.astype(F32)).astype(BF16)
+    top = x[80:].astype(BF16).astype(F32)
+    last = jnp.concatenate([top, x[80:] - top], axis=0).astype(BF16)
+    return high, low, last
+
+
+def join_solid(y):
+    return jnp.concatenate([y[:80] + y[80:160], y[160:168] + y[168:176]], axis=0)
+
+
 def solid_weights(x0, x1, x2):
-    k = rows_of((32, 1))
-    return pick_basis(x0, k // 9) * pick_basis(x1, (k // 3) % 3) * pick_basis(x2, k % 3)
+    j = rows_of((8, 1))
+    plane = pick_basis(x1, j // 3) * pick_basis(x2, j % 3)
+    corner = (0.5 * x1 * x1) * (0.5 * x2 * x2)
+    b0 = 0.5 * (1.0 - x0) ** 2
+    b1 = 0.5 * (1.0 + 2.0 * x0 - 2.0 * x0 * x0)
+    b2 = 0.5 * x0 * x0
+    tiles = [plane * b0, plane * b1, plane * b2]
+    return tiles, pick_basis(x0, j % 3) * corner, b2 * corner
 
 
 def shell_weights(x0, x1):
@@ -120,10 +138,13 @@
     for k in range(peers):
         part_ref[k, 0:14, 0:own] = tight[0:14, k * own : (k + 1) * own]
         part_ref[k, 0:13, own:] = tight[14:27, k * own : (k + 1) * own]
-    wide[...] = jnp.zeros_like(wide)
+    wide[80:88] = jnp.zeros((8, wide.shape[1]), F32)
     for c in range(3):
-        wide[c * 32 : c * 32 + 27, :] = coef_ref[c * 27 : c * 27 + 27, :]
-    table_ref[...] = split(wide[...])
+        for a in range(3):
+            k = c * 27 + a * 9
+            wide[c * 24 + a * 8 : c * 24 + a * 8 + 8, :] = coef_ref[k : k + 8, :]
+            wide[72 + c * 3 + a : 73 + c * 3 + a, :] = coef_ref[k + 8 : k + 9, :]
+    table_ref[0:80], table_ref[80:160], table_ref[160:176] = split_solid(wide[...])
 
 
 def force_kernel(recv_ref, table_ref, part_ref, back_ref, beside_ref, across_ref):
@@ -133,11 +154,16 @@
         point = recv_ref[g]
         index = point[0:1].astype(I32) - 1
         picked = dot(table_ref[...], one_hot(index, elements), NN)
-        picked = picked[:96] + picked[96:]
-        w = solid_weights(point[1:2], point[2:3], point[3:4])
-        speed = [
-            jnp.sum(picked[c * 32 : c * 32 + 32] * w, axis=0, keepdims=True) for c in range(3)
-        ]
+        picked = join_solid(picked)
+        tiles, rest, final = solid_weights(point[1:2], point[2:3], point[3:4])
+        rest = picked[72:80] * rest
+        speed = []
+        for c in range(3):
+            part = jnp.where(rows_of((8, 1)) // 3 == c, rest, 0.0)
+            for a in range(3):
+                part = part + picked[c * 24 + a * 8 : c * 24 + a * 8 + 8] * tiles[a]
+            speed.append(jnp.sum(part, axis=0, keepdims=True))
+        speed[2] = speed[2] + picked[80:81] * final
         scale = BETA * point[7:8]
         beside_ref[g * 8 : g * 8 + 4] = point[0:4]
         for c in range(3):
@@ -159,9 +185,16 @@
     for g in range(groups):
         point = source_ref[g * 8 : (g + 1) * 8]
         index.append(point[0:1].astype(I32))
-        w = solid_weights(point[1:2], point[2:3], point[3:4])
-        part = jnp.concatenate([w * point[4 + c : 5 + c] for c in range(3)], axis=0)
-        terms[:, g * GROUP : (g + 1) * GROUP] = split(part)
+        tiles, rest, final = solid_weights(point[1:2], point[2:3], point[3:4])
+        f = [point[4 + c : 5 + c] for c in range(3)]
+        which = rows_of((8, 1)) // 3
+        parts = [tile * f[c] for c in range(3) for tile in tiles]
+        parts.append(rest * jnp.where(which == 0, f[0], jnp.where(which == 1, f[1], f[2])))
+        parts.append(jnp.broadcast_to(final * f[2], (8, GROUP)))
+        here = pl.ds(g * GROUP, GROUP)
+        terms[0:80, here], terms[80:160, here], terms[160:176, here] = split_solid(
+            jnp.concatenate(parts, axis=0)
+        )
     return dot(terms[...], one_hot(jnp.concatenate(index, axis=1), rows, first), NT)
 
 
@@ -171,7 +204,7 @@
     first = me_ref[0] * rows + 1
     total = spread(own_ref, terms, first, rows)
     total = total + spread(across_ref, terms, first, rows)
-    total_ref[...] = total[:96] + total[96:]
+    total_ref[...] = join_solid(total)
     patch_ref[...] = part_ref[0] + across_ref[tail : tail + 16]
 
 
@@ -182,9 +215,12 @@
     first = me_ref[0] * rows + 1
     total = spread(beside_ref, terms, first, rows)
     total = total + spread(corner_ref, terms, first, rows)
-    total = total_ref[...] + total[:96] + total[96:]
+    total = total_ref[...] + join_solid(total)
     for c in range(3):
-        flow_ref[c * 27 : c * 27 + 27, :] = total[c * 32 : c * 32 + 27]
+        for a in range(3):
+            k = c * 27 + a * 9
+            flow_ref[k : k + 8, :] = total[c * 24 + a * 8 : c * 24 + a * 8 + 8]
+            flow_ref[k + 8 : k + 9, :] = total[72 + c * 3 + a : 73 + c * 3 + a]
     part = part_ref[...] + beside_ref[tail:] + corner_ref[tail + 16 :]
     patch_ref[0:14] = part[0:14, 0:own]
     patch_ref[14:27] = part[0:13, own:]
@@ -268,11 +304,11 @@
     ctrl = (here, twin, far, diag)
     pushes, part, table = call(
         functools.partial(contact_kernel, peers=peers),
-        [shape(3, count), shape(peers, 16, 2 * own), shape(192, elements, dtype=BF16)],
+        [shape(3, count), shape(peers, 16, 2 * own), shape(176, elements, dtype=BF16)],
         scratch=[
             pltpu.VMEM((48, peers * own), F32),
             pltpu.VMEM((32, peers * own), F32),
-            pltpu.VMEM((96, elements), F32),
+            pltpu.VMEM((88, elements), F32),
         ],
         smem=1,
         operands=(me, *ctrl, contact_patch.reshape(1, count), contact_param, gp_pos, vel_coef),
@@ -292,8 +328,8 @@
     rows = elements // peers
     total, patch_part = call(
         near_kernel,
-        [shape(96, rows), shape(16, 2 * own)],
-        scratch=[pltpu.VMEM((192, width), BF16)],
+        [shape(88, rows), shape(16, 2 * own)],
+        scratch=[pltpu.VMEM((176, width), BF16)],
         smem=1,
         operands=(me, beside, from_across, part),
         flops=2 * 10**9,
@@ -301,7 +337,7 @@
     flow_force, patch_force = call(
         last_kernel,
         [shape(81, rows), shape(27, own)],
-        scratch=[pltpu.VMEM((192, width), BF16)],
+        scratch=[pltpu.VMEM((176, width), BF16)],
         smem=1,
         operands=(me, from_beside, from_corner, total, patch_part),
         flops=2 * 10**9,

time: 42.4 us -> 42.1 us (level)
  Pallas kernels: 13.2 us -> 12.6 us
    pallas_call x6, Pallas kernels: 13.2 us -> 12.6 us  [call(): pl.pallas_call(kernel, out_shape=out_shape, in_specs=specs, out_specs=jax...]
  transfers between devices with their start and end apart: 8 -> 8, of which waited for: 5 -> 5; matrix products, arithmetic and copies ran while one was open for 0% -> 0% of each run, Pallas kernels for 14% -> 13%
where the time goes in v2:
time: 42.1 us; the launch traced here: 41.7 us
  starting transfers between devices  16.7 us (40%)
  Pallas kernels  12.6 us (30%)
  waiting for transfers between devices  11.7 us (28%)
  between operations  0.73 us (2%)
    pallas_call x6, Pallas kernels, call(): pl.pallas_call(kernel, out_shape=out_shape, in_specs=specs, out_specs=jax...  12.6 us
    ppermute x6, waiting for transfers between devices, swap(): return lax.ppermute(x, 'leaf', [(i, i ^ k) for i in range(peers)])  8.41 us
    all_to_all x1, starting transfers between devices, per_device(): lax.all_to_all(payload, 'flow', split_axis=0, concat_axis=0, tiled=True)  7.43 us
    all_to_all x1, starting transfers between devices, per_device(): lax.all_to_all(to_owners(force), 'flow', split_axis=0, concat_axis=0, til...  5.98 us
    ppermute x6, starting transfers between devices, swap(): return lax.ppermute(x, 'leaf', [(i, i ^ k) for i in range(peers)])  3.34 us
    all_to_all x1, waiting for transfers between devices, per_device(): lax.all_to_all(to_owners(force), 'flow', split_axis=0, concat_axis=0, til...  2.6 us
  transfers between devices with their start and end apart: 8, of which 5 were waited for; matrix products, arithmetic and copies ran while one was open for 0% of the time, Pallas kernels for 13%

profile of v2, /device:TPU:0, one launch (start us, length us, event | category | flops | bytes accessed | tf_op | source)
XLA Modules:
  0.0 41.7 jit_solution(10396618446592991079)
XLA Ops:
  0.6 2.2 %shard_map.121 = (f32[8,8,512]{2,1,0:T(8,128)}, s32[1,2048]{1,0:T(1,128)}) custom-call(s32[1,2048]{1,0:T(1,128)} %bitcast.6, s32[1,2048]{1,0:T(1,128)} %bitcast.8, f32[3,2048]{1,0:T(4,128)} %param_ref.1, f32[3,2048]{1,0:T(4,128)} %vel_ref.1, f32[1,2048]{1,0:T(1,128)} %bitcast.9), custom_call_target="tpu_custom_call" | custom-call | flops 1000000000 | tf_op jit(solution)/shard_map/pallas_call | solution.py:248
  2.9 7.4 %all-to-all-start = ((f32[8,8,512]{2,1,0:T(8,128)}), f32[8,8,512]{2,1,0:T(8,128)S(1)}, u32[]{:S(2)}, u32[]{:S(2)}) async-start(f32[8,8,512]{2,1,0:T(8,128)} %get-tuple-element.20), calls=%async_computation | async-start | bytes 262144 | tf_op jit(solution)/shard_map/all_to_all | solution.py:301
  10.3 0.0 copy-start.4
  10.3 1.6 %collective-permute-start.1 = (f32[27,256]{1,0:T(8,128)S(1)}, f32[27,256]{1,0:T(8,128)S(1)}, u32[]{:S(2)}, u32[]{:S(2)}) collective-permute-start(f32[27,256]{1,0:T(8,128)S(1)} %copy-done.1), channel_id=1, source_target_pairs={{0,2},{1,3},{2,0},{3,1},{4,6},{5,7},{6,4},{7,5},{8,10},{9,11},{10,... | collective-permute-start | bytes 82952 | tf_op jit(solution)/shard_map/ppermute | solution.py:278
  11.9 0.0 collective-permute-start
  11.9 2.4 %collective-permute-done.1.refs_2_ = f32[27,256]{1,0:T(8,128)S(1)} collective-permute-done((f32[27,256]{1,0:T(8,128)S(1)}, f32[27,256]{1,0:T(8,128)S(1)}, u32[]{:S(2)}, u32[]{:S(2)}) %collective-permute-start.1) | collective-permute-done | bytes 27680 | tf_op jit(solution)/shard_map/ppermute | solution.py:278
  14.3 0.0 collective-permute-start.2
  14.3 0.0 collective-permute-done.refs_1_
  14.3 1.2 %collective-permute-done.2.refs_3_ = f32[27,256]{1,0:T(8,128)S(1)} collective-permute-done((f32[27,256]{1,0:T(8,128)S(1)}, f32[27,256]{1,0:T(8,128)S(1)}, u32[]{:S(2)}, u32[]{:S(2)}) %collective-permute-start.2) | collective-permute-done | bytes 27680 | tf_op jit(solution)/shard_map/ppermute | solution.py:278
  15.5 1.5 %shard_map.122 = (f32[3,2048]{1,0:T(4,128)S(1)}, f32[4,16,512]{2,1,0:T(8,128)S(1)}, bf16[176,2048]{1,0:T(8,128)(2,1)S(1)}) custom-call(s32[1]{0:T(128)} %bitcast.me_ref, f32[27,256]{1,0:T(8,128)S(1)} %copy-done.1, f32[27,256]{1,0:T(8,128)S(1)} %collective-permute-done.refs_1_, f32[27,256]{1,0:T(8,128)S(1)} %collective-permute-done.1.refs_2_, ...), custom_call_target="tpu_custom_call" | custom-call | flops 1000000000 | tf_op jit(solution)/shard_map/pallas_call | solution.py:248
  17.0 0.6 %all-to-all-done.recv_ref = f32[8,8,512]{2,1,0:T(8,128)S(1)} async-done(((f32[8,8,512]{2,1,0:T(8,128)}), f32[8,8,512]{2,1,0:T(8,128)S(1)}, u32[]{:S(2)}, u32[]{:S(2)}) %all-to-all-start) | async-done | bytes 131104 | tf_op jit(solution)/shard_map/all_to_all | solution.py:301
  17.6 3.9 %shard_map.123 = (f32[8,4,512]{2,1,0:T(4,128)}, f32[80,512]{1,0:T(8,128)S(1)}, f32[96,512]{1,0:T(8,128)S(1)}) custom-call(f32[8,8,512]{2,1,0:T(8,128)S(1)} %all-to-all-done.recv_ref, bf16[176,2048]{1,0:T(8,128)(2,1)S(1)} %get-tuple-element.22.table_ref, f32[4,16,512]{2,1,0:T(8,128)S(1)} %get-tuple-element.23.part_ref), custom_call_target="tpu_custom_call" | custom-call | flops 4000000000 | tf_op jit(solution)/shard_map/pallas_call | solution.py:248
  21.5 1.5 %collective-permute-start.4 = (f32[96,512]{1,0:T(8,128)S(1)}, f32[96,512]{1,0:T(8,128)S(1)}, u32[]{:S(2)}, u32[]{:S(2)}) collective-permute-start(f32[96,512]{1,0:T(8,128)S(1)} %get-tuple-element.25), channel_id=1, source_target_pairs={{0,2},{1,3},{2,0},{3,1},{4,6},{5,7},{6,4},{7,5},{8,10},{9,11},{10,... | collective-permute-start | bytes 589832 | tf_op jit(solution)/shard_map/ppermute | solution.py:278
  23.1 4.8 %collective-permute-done.4.across_ref = f32[96,512]{1,0:T(8,128)S(1)} collective-permute-done((f32[96,512]{1,0:T(8,128)S(1)}, f32[96,512]{1,0:T(8,128)S(1)}, u32[]{:S(2)}, u32[]{:S(2)}) %collective-permute-start.4) | collective-permute-done | bytes 196640 | tf_op jit(solution)/shard_map/ppermute | solution.py:278
  27.9 0.0 collective-permute-start.5
  27.9 6.0 %all-to-all-start.1 = ((f32[8,4,512]{2,1,0:T(4,128)}), f32[8,4,512]{2,1,0:T(4,128)S(1)}, u32[]{:S(2)}, u32[]{:S(2)}) async-start(f32[8,4,512]{2,1,0:T(4,128)} %get-tuple-element.31), calls=%async_computation.1 | async-start | bytes 131072 | tf_op jit(solution)/shard_map/all_to_all | solution.py:325
  33.9 0.2 collective-permute-start.3
  34.1 1.7 %shard_map.124 = (f32[88,512]{1,0:T(8,128)S(1)}, f32[16,512]{1,0:T(8,128)S(1)}) custom-call(s32[1]{0:T(128)} %bitcast.me_ref, f32[80,512]{1,0:T(8,128)S(1)} %get-tuple-element.24.own_ref, f32[96,512]{1,0:T(8,128)S(1)} %collective-permute-done.4.across_ref, f32[4,16,512]{2,1,0:T(8,128)S(1)} %get-tuple-element.23.part_ref), custom_call_target="tpu_custom_call" | custom-call | flops 2000000000 | tf_op jit(solution)/shard_map/pallas_call | solution.py:248
  35.8 0.0 collective-permute-done.3.beside_ref
  35.8 0.0 copy-start.5
  35.8 0.0 copy-start.6
  35.8 2.4 %shard_map.125 = (f32[81,512]{1,0:T(8,128)}, f32[27,256]{1,0:T(8,128)}) custom-call(s32[1]{0:T(128)} %bitcast.me_ref, f32[80,512]{1,0:T(8,128)S(1)} %collective-permute-done.3.beside_ref, f32[96,512]{1,0:T(8,128)S(1)} %collective-permute-done.5.corner_ref, f32[88,512]{1,0:T(8,128)S(1)} %get-tuple-element.26.total_ref, f32[16,512]{1,0:T(8,128)S(1)} %get-tuple-element.27.part_ref), custom_call_target="tpu_custom_call" | custom-call | flops 2000000000 | tf_op jit(solution)/shard_map/pallas_call | solution.py:248
  38.2 2.6 %all-to-all-done.1.back_ref = f32[8,4,512]{2,1,0:T(4,128)S(1)} async-done(((f32[8,4,512]{2,1,0:T(4,128)}), f32[8,4,512]{2,1,0:T(4,128)S(1)}, u32[]{:S(2)}, u32[]{:S(2)}) %all-to-all-start.1) | async-done | bytes 65568 | tf_op jit(solution)/shard_map/all_to_all | solution.py:325
  40.8 1.0 %shard_map.126 = f32[3,2048]{1,0:T(4,128)} custom-call(f32[8,4,512]{2,1,0:T(4,128)S(1)} %all-to-all-done.1.back_ref, s32[1,2048]{1,0:T(1,128)S(1)} %bitcast.7, s32[1,2048]{1,0:T(1,128)S(1)} %copy-done.6, f32[3,2048]{1,0:T(4,128)S(1)} %get-tuple-element.33.push_ref), custom_call_target="tpu_custom_call" | custom-call | flops 100000000 | tf_op jit(solution)/shard_map/pallas_call | solution.py:248
  (12 shorter events, 0.0 us)
Async XLA Ops:
  0.6 14.9 %copy-start = (f32[81,2048]{1,0:T(8,128)S(1)}, f32[81,2048]{1,0:T(8,128)}, u32[]{:S(2)}) copy-start(f32[81,2048]{1,0:T(8,128)} %refs_7_.1) | copy-start | bytes 1990660
  2.8 7.4 %copy-start.1 = (f32[27,256]{1,0:T(8,128)S(1)}, f32[27,256]{1,0:T(8,128)}, u32[]{:S(2)}) copy-start(f32[27,256]{1,0:T(8,128)} %refs_0_) | copy-start | bytes 82948
  2.8 12.7 %copy-start.2 = (f32[3,2048]{1,0:T(4,128)S(1)}, f32[3,2048]{1,0:T(4,128)}, u32[]{:S(2)}) copy-start(f32[3,2048]{1,0:T(4,128)} %refs_6_.1) | copy-start | bytes 73732
  2.8 12.7 %copy-start.3 = (f32[2,2048]{1,0:T(2,128)S(1)}, f32[2,2048]{1,0:T(2,128)}, u32[]{:S(2)}) copy-start(f32[2,2048]{1,0:T(2,128)} %refs_5_.1) | copy-start | bytes 49156
  2.9 14.8 %all-to-all-start = ((f32[8,8,512]{2,1,0:T(8,128)}), f32[8,8,512]{2,1,0:T(8,128)S(1)}, u32[]{:S(2)}, u32[]{:S(2)}) async-start(f32[8,8,512]{2,1,0:T(8,128)} %get-tuple-element.20), calls=%async_computation | async-start | bytes 262144 | tf_op jit(solution)/shard_map/all_to_all | solution.py:301
  10.3 5.2 %copy-start.4 = (s32[2048]{0:T(1024)S(1)}, s32[2048]{0:T(1024)}, u32[]{:S(2)}) copy-start(s32[2048]{0:T(1024)} %param.17) | copy-start | bytes 24580
  10.3 4.0 %collective-permute-start.1 = (f32[27,256]{1,0:T(8,128)S(1)}, f32[27,256]{1,0:T(8,128)S(1)}, u32[]{:S(2)}, u32[]{:S(2)}) collective-permute-start(f32[27,256]{1,0:T(8,128)S(1)} %copy-done.1), channel_id=1, source_target_pairs={{0,2},{1,3},{2,0},{3,1},{4,6},{5,7},{6,4},{7,5},{8,10},{9,11},{10,... | collective-permute-start | bytes 82952 | tf_op jit(solution)/shard_map/ppermute | solution.py:278
  11.9 2.4 %collective-permute-start = (f32[27,256]{1,0:T(8,128)S(1)}, f32[27,256]{1,0:T(8,128)S(1)}, u32[]{:S(2)}, u32[]{:S(2)}) collective-permute-start(f32[27,256]{1,0:T(8,128)S(1)} %copy-done.1), channel_id=1, source_target_pairs={{0,1},{1,0},{2,3},{3,2},{4,5},{5,4},{6,7},{7,6},{8,9},{9,8},{10,11... | collective-permute-start | bytes 82952 | tf_op jit(solution)/shard_map/ppermute | solution.py:278
  14.3 1.2 %collective-permute-start.2 = (f32[27,256]{1,0:T(8,128)S(1)}, f32[27,256]{1,0:T(8,128)S(1)}, u32[]{:S(2)}, u32[]{:S(2)}) collective-permute-start(f32[27,256]{1,0:T(8,128)S(1)} %collective-permute-done.1.refs_2_), channel_id=1, source_target_pairs={{0,1},{1,0},{2,3},{3,2},{4,5},{5,4},{6,7},{7,6},{8,9},{9,8},{10,11... | collective-permute-start | bytes 82952 | tf_op jit(solution)/shard_map/ppermute | solution.py:278
  21.5 6.3 %collective-permute-start.4 = (f32[96,512]{1,0:T(8,128)S(1)}, f32[96,512]{1,0:T(8,128)S(1)}, u32[]{:S(2)}, u32[]{:S(2)}) collective-permute-start(f32[96,512]{1,0:T(8,128)S(1)} %get-tuple-element.25), channel_id=1, source_target_pairs={{0,2},{1,3},{2,0},{3,1},{4,6},{5,7},{6,4},{7,5},{8,10},{9,11},{10,... | collective-permute-start | bytes 589832 | tf_op jit(solution)/shard_map/ppermute | solution.py:278
  27.9 7.9 %collective-permute-start.5 = (f32[96,512]{1,0:T(8,128)S(1)}, f32[96,512]{1,0:T(8,128)S(1)}, u32[]{:S(2)}, u32[]{:S(2)}) collective-permute-start(f32[96,512]{1,0:T(8,128)S(1)} %collective-permute-done.4.across_ref), channel_id=1, source_target_pairs={{0,1},{1,0},{2,3},{3,2},{4,5},{5,4},{6,7},{7,6},{8,9},{9,8},{10,11... | collective-permute-start | bytes 589832 | tf_op jit(solution)/shard_map/ppermute | solution.py:278
  27.9 12.9 %all-to-all-start.1 = ((f32[8,4,512]{2,1,0:T(4,128)}), f32[8,4,512]{2,1,0:T(4,128)S(1)}, u32[]{:S(2)}, u32[]{:S(2)}) async-start(f32[8,4,512]{2,1,0:T(4,128)} %get-tuple-element.31), calls=%async_computation.1 | async-start | bytes 131072 | tf_op jit(solution)/shard_map/all_to_all | solution.py:325
  33.9 1.9 %collective-permute-start.3 = (f32[80,512]{1,0:T(8,128)S(1)}, f32[80,512]{1,0:T(8,128)S(1)}, u32[]{:S(2)}, u32[]{:S(2)}) collective-permute-start(f32[80,512]{1,0:T(8,128)S(1)} %get-tuple-element.24.own_ref), channel_id=1, source_target_pairs={{0,1},{1,0},{2,3},{3,2},{4,5},{5,4},{6,7},{7,6},{8,9},{9,8},{10,11... | collective-permute-start | bytes 491528 | tf_op jit(solution)/shard_map/ppermute | solution.py:278
  35.8 5.0 %copy-start.5 = (s32[2048,1]{0,1:T(1,128)S(1)}, s32[2048,1]{0,1:T(1,128)}, u32[]{:S(2)}) copy-start(s32[2048,1]{0,1:T(1,128)} %param.11) | copy-start | bytes 24580
  35.8 5.0 %copy-start.6 = (s32[1,2048]{1,0:T(1,128)S(1)}, s32[1,2048]{1,0:T(1,128)}, u32[]{:S(2)}) copy-start(s32[1,2048]{1,0:T(1,128)} %get-tuple-element.32.rank_ref) | copy-start | bytes 24580

commit v3 on v2

--- a/solution.py
+++ b/solution.py
@@ -147,32 +147,48 @@
     table_ref[0:80], table_ref[80:160], table_ref[160:176] = split_solid(wide[...])
 
 
-def force_kernel(recv_ref, table_ref, part_ref, back_ref, beside_ref, across_ref):
+def force_of(point, table_ref):
+    index = point[0:1].astype(I32) - 1
+    picked = join_solid(dot(table_ref[...], one_hot(index, table_ref.shape[1]), NN))
+    tiles, rest, final = solid_weights(point[1:2], point[2:3], point[3:4])
+    rest = picked[72:80] * rest
+    forces = []
+    for c in range(3):
+        part = jnp.where(rows_of((8, 1)) // 3 == c, rest, 0.0)
+        for a in range(3):
+            part = part + picked[c * 24 + a * 8 : c * 24 + a * 8 + 8] * tiles[a]
+        speed = jnp.sum(part, axis=0, keepdims=True)
+        if c == 2:
+            speed = speed + picked[80:81] * final
+        forces.append(BETA * point[7:8] * (point[4 + c : 5 + c] - speed))
+    return forces
+
+
+def home_kernel(row_ref, sent_ref, table_ref, out_ref):
+    for c, force in enumerate(force_of(sent_ref[row_ref[0]], table_ref)):
+        out_ref[c : c + 1] = force
+    out_ref[3:8] = jnp.zeros((5, GROUP), F32)
+
+
+def force_kernel(row_ref, recv_ref, table_ref, part_ref, *refs):
+    *homes, back_ref, beside_ref, across_ref = refs
     groups = recv_ref.shape[0]
-    elements = table_ref.shape[1]
-    for g in range(groups):
+
+    def put(g, point, forces):
+        both = jnp.concatenate([point[0:4], *forces, jnp.zeros((1, GROUP), F32)], axis=0)
+        here = pl.ds(pl.multiple_of(g * 8, 8), 8)
+        beside_ref[here] = both
+        across_ref[here] = both
+        back_ref[g] = both[4:8]
+
+    first = row_ref[0]
+    for r in range(groups):
+        g = lax.rem(first + r, groups)
         point = recv_ref[g]
-        index = point[0:1].astype(I32) - 1
-        picked = dot(table_ref[...], one_hot(index, elements), NN)
-        picked = join_solid(picked)
-        tiles, rest, final = solid_weights(point[1:2], point[2:3], point[3:4])
-        rest = picked[72:80] * rest
-        speed = []
-        for c in range(3):
-            part = jnp.where(rows_of((8, 1)) // 3 == c, rest, 0.0)
-            for a in range(3):
-                part = part + picked[c * 24 + a * 8 : c * 24 + a * 8 + 8] * tiles[a]
-            speed.append(jnp.sum(part, axis=0, keepdims=True))
-        speed[2] = speed[2] + picked[80:81] * final
-        scale = BETA * point[7:8]
-        beside_ref[g * 8 : g * 8 + 4] = point[0:4]
-        for c in range(3):
-            force = scale * (point[4 + c : 5 + c] - speed[c])
-            beside_ref[g * 8 + 4 + c : g * 8 + 5 + c] = force
-            back_ref[g, c : c + 1] = force
-        beside_ref[g * 8 + 7 : g * 8 + 8] = jnp.zeros((1, GROUP), F32)
-        back_ref[g, 3:4] = jnp.zeros((1, GROUP), F32)
-        across_ref[g * 8 : (g + 1) * 8] = beside_ref[g * 8 : (g + 1) * 8]
+        if homes and r == 0:
+            put(g, point, [homes[0][c : c + 1] for c in range(3)])
+        else:
+            put(g, point, force_of(point, table_ref))
     tail = groups * 8
     beside_ref[tail:] = part_ref[1]
     across_ref[tail : tail + 16] = part_ref[2]
@@ -315,10 +331,20 @@
         flops=10**9,
     )
     tail = groups * 8
+    row = lax.axis_index("flow").astype(I32).reshape(1) % groups
+    homes = ()
+    if slots == GROUP:
+        homes = (
+            call(
+                home_kernel, shape(8, GROUP), smem=1,
+                operands=(row, payload, table), flops=10**9,
+            ),
+        )
     force, beside, across = call(
         force_kernel,
         [shape(groups, 4, GROUP), shape(tail + 16, GROUP), shape(tail + 32, GROUP)],
-        operands=(to_groups(recv), table, part),
+        smem=1,
+        operands=(row, to_groups(recv), table, part, *homes),
         flops=4 * 10**9,
     )
     from_across = swap(across, 2)

time: 42.1 us -> 40.2 us (0.955)
  starting transfers between devices: 16.7 us -> 13.9 us
  waiting for transfers between devices: 11.7 us -> 12.4 us
    all_to_all x1, waiting for transfers between devices: 0.64 us -> 3.81 us  [per_device(): lax.all_to_all(payload, 'flow', split_axis=0, concat_axis=0, tiled=True)]
    ppermute x6, waiting for transfers between devices: 8.41 us -> 6.03 us  [swap(): return lax.ppermute(x, 'leaf', [(i, i ^ k) for i in range(peers)])]
    all_to_all x1, starting transfers between devices: 5.98 us -> 3.63 us  [per_device(): lax.all_to_all(to_owners(force), 'flow', split_axis=0, concat_axis=0, til...]
    all_to_all x1, starting transfers between devices: 7.43 us -> 5.94 us  [per_device(): lax.all_to_all(payload, 'flow', split_axis=0, concat_axis=0, tiled=True)]
    ppermute x6, starting transfers between devices: 3.34 us -> 4.36 us  [swap(): return lax.ppermute(x, 'leaf', [(i, i ^ k) for i in range(peers)])]
    pallas_call x6 -> x7, Pallas kernels: 12.6 us -> 12.8 us  [call(): pl.pallas_call(kernel, out_shape=out_shape, in_specs=specs, out_specs=jax...]
  transfers between devices with their start and end apart: 8 -> 8, of which waited for: 5 -> 5; matrix products, arithmetic and copies ran while one was open for 0% -> 0% of each run, Pallas kernels for 13% -> 15%
where the time goes in v3:
time: 40.2 us; the launch traced here: 39.8 us
  starting transfers between devices  13.9 us (35%)
  Pallas kernels  12.8 us (32%)
  waiting for transfers between devices  12.4 us (31%)
  between operations  0.75 us (2%)
    pallas_call x7, Pallas kernels, call(): pl.pallas_call(kernel, out_shape=out_shape, in_specs=specs, out_specs=jax...  12.8 us
    ppermute x6, waiting for transfers between devices, swap(): return lax.ppermute(x, 'leaf', [(i, i ^ k) for i in range(peers)])  6.03 us
    all_to_all x1, starting transfers between devices, per_device(): lax.all_to_all(payload, 'flow', split_axis=0, concat_axis=0, tiled=True)  5.94 us
    ppermute x6, starting transfers between devices, swap(): return lax.ppermute(x, 'leaf', [(i, i ^ k) for i in range(peers)])  4.36 us
    all_to_all x1, waiting for transfers between devices, per_device(): lax.all_to_all(payload, 'flow', split_axis=0, concat_axis=0, tiled=True)  3.81 us
    all_to_all x1, starting transfers between devices, per_device(): lax.all_to_all(to_owners(force), 'flow', split_axis=0, concat_axis=0, til...  3.63 us
    all_to_all x1, waiting for transfers between devices, per_device(): lax.all_to_all(to_owners(force), 'flow', split_axis=0, concat_axis=0, til...  2.53 us
  transfers between devices with their start and end apart: 8, of which 5 were waited for; matrix products, arithmetic and copies ran while one was open for 0% of the time, Pallas kernels for 15%

profile of v3, /device:TPU:0, one launch (start us, length us, event | category | flops | bytes accessed | tf_op | source)
XLA Modules:
  0.0 39.8 jit_solution(4586816174883161927)
XLA Ops:
  0.7 2.2 %shard_map.121 = (f32[8,8,512]{2,1,0:T(8,128)}, s32[1,2048]{1,0:T(1,128)}) custom-call(s32[1,2048]{1,0:T(1,128)} %bitcast.7, s32[1,2048]{1,0:T(1,128)} %bitcast.9, f32[3,2048]{1,0:T(4,128)} %param_ref.1, f32[3,2048]{1,0:T(4,128)} %vel_ref.1, f32[1,2048]{1,0:T(1,128)} %bitcast.10), custom_call_target="tpu_custom_call" | custom-call | flops 1000000000 | tf_op jit(solution)/shard_map/pallas_call | solution.py:264
  2.9 3.0 %collective-permute-start.1 = (f32[27,256]{1,0:T(8,128)S(1)}, f32[27,256]{1,0:T(8,128)S(1)}, u32[]{:S(2)}, u32[]{:S(2)}) collective-permute-start(f32[27,256]{1,0:T(8,128)S(1)} %copy-done.2), channel_id=1, source_target_pairs={{0,2},{1,3},{2,0},{3,1},{4,6},{5,7},{6,4},{7,5},{8,10},{9,11},{10,... | collective-permute-start | bytes 82952 | tf_op jit(solution)/shard_map/ppermute | solution.py:294
  5.9 5.9 %all-to-all-start = ((f32[8,8,512]{2,1,0:T(8,128)}), f32[8,8,512]{2,1,0:T(8,128)S(1)}, u32[]{:S(2)}, u32[]{:S(2)}) async-start(f32[8,8,512]{2,1,0:T(8,128)} %get-tuple-element.20.sent_ref), calls=%async_computation | async-start | bytes 262144 | tf_op jit(solution)/shard_map/all_to_all | solution.py:317
  11.8 0.1 collective-permute-start
  11.9 0.5 %collective-permute-start.2 = (f32[27,256]{1,0:T(8,128)S(1)}, f32[27,256]{1,0:T(8,128)S(1)}, u32[]{:S(2)}, u32[]{:S(2)}) collective-permute-start(f32[27,256]{1,0:T(8,128)S(1)} %collective-permute-done.1.refs_2_), channel_id=1, source_target_pairs={{0,1},{1,0},{2,3},{3,2},{4,5},{5,4},{6,7},{7,6},{8,9},{9,8},{10,11... | collective-permute-start | bytes 82952 | tf_op jit(solution)/shard_map/ppermute | solution.py:294
  12.4 0.7 %collective-permute-done.refs_1_ = f32[27,256]{1,0:T(8,128)S(1)} collective-permute-done((f32[27,256]{1,0:T(8,128)S(1)}, f32[27,256]{1,0:T(8,128)S(1)}, u32[]{:S(2)}, u32[]{:S(2)}) %collective-permute-start) | collective-permute-done | bytes 27680 | tf_op jit(solution)/shard_map/ppermute | solution.py:294
  13.1 0.2 collective-permute-done.2.refs_3_
  13.3 0.0 copy-start
  13.3 1.5 %shard_map.122 = (f32[3,2048]{1,0:T(4,128)S(1)}, f32[4,16,512]{2,1,0:T(8,128)S(1)}, bf16[176,2048]{1,0:T(8,128)(2,1)S(1)}) custom-call(s32[1]{0:T(128)} %bitcast.me_ref, f32[27,256]{1,0:T(8,128)S(1)} %copy-done.2, f32[27,256]{1,0:T(8,128)S(1)} %collective-permute-done.refs_1_, f32[27,256]{1,0:T(8,128)S(1)} %collective-permute-done.1.refs_2_, ...), custom_call_target="tpu_custom_call" | custom-call | flops 1000000000 | tf_op jit(solution)/shard_map/pallas_call | solution.py:264
  14.8 0.6 %shard_map.123.refs_0_ = f32[8,512]{1,0:T(8,128)S(1)} custom-call(s32[1]{0:T(128)S(6)} %select_n.7.row_ref, f32[8,8,512]{2,1,0:T(8,128)S(1)} %copy-done, bf16[176,2048]{1,0:T(8,128)(2,1)S(1)} %get-tuple-element.22.table_ref), custom_call_target="tpu_custom_call" | custom-call | flops 1000000000 | tf_op jit(solution)/shard_map/pallas_call | solution.py:264
  15.3 3.8 %all-to-all-done.recv_ref = f32[8,8,512]{2,1,0:T(8,128)S(1)} async-done(((f32[8,8,512]{2,1,0:T(8,128)}), f32[8,8,512]{2,1,0:T(8,128)S(1)}, u32[]{:S(2)}, u32[]{:S(2)}) %all-to-all-start) | async-done | bytes 131104 | tf_op jit(solution)/shard_map/all_to_all | solution.py:317
  19.1 3.5 %shard_map.124 = (f32[8,4,512]{2,1,0:T(4,128)}, f32[80,512]{1,0:T(8,128)S(1)}, f32[96,512]{1,0:T(8,128)S(1)}) custom-call(s32[1]{0:T(128)S(6)} %select_n.7.row_ref, f32[8,8,512]{2,1,0:T(8,128)S(1)} %all-to-all-done.recv_ref, bf16[176,2048]{1,0:T(8,128)(2,1)S(1)} %get-tuple-element.22.table_ref, f32[4,16,512]{2,1,0:T(8,128)S(1)} %get-tuple-element.23.part_ref, ...), custom_call_target="tpu_custom_call" | custom-call | flops 4000000000 | tf_op jit(solution)/shard_map/pallas_call | solution.py:264
  22.7 0.5 %collective-permute-start.4 = (f32[96,512]{1,0:T(8,128)S(1)}, f32[96,512]{1,0:T(8,128)S(1)}, u32[]{:S(2)}, u32[]{:S(2)}) collective-permute-start(f32[96,512]{1,0:T(8,128)S(1)} %get-tuple-element.25), channel_id=1, source_target_pairs={{0,2},{1,3},{2,0},{3,1},{4,6},{5,7},{6,4},{7,5},{8,10},{9,11},{10,... | collective-permute-start | bytes 589832 | tf_op jit(solution)/shard_map/ppermute | solution.py:294
  23.2 5.2 %collective-permute-done.4.across_ref = f32[96,512]{1,0:T(8,128)S(1)} collective-permute-done((f32[96,512]{1,0:T(8,128)S(1)}, f32[96,512]{1,0:T(8,128)S(1)}, u32[]{:S(2)}, u32[]{:S(2)}) %collective-permute-start.4) | collective-permute-done | bytes 196640 | tf_op jit(solution)/shard_map/ppermute | solution.py:294
  28.3 0.0 collective-permute-start.5
  28.3 3.6 %all-to-all-start.1 = ((f32[8,4,512]{2,1,0:T(4,128)}), f32[8,4,512]{2,1,0:T(4,128)S(1)}, u32[]{:S(2)}, u32[]{:S(2)}) async-start(f32[8,4,512]{2,1,0:T(4,128)} %get-tuple-element.31), calls=%async_computation.1 | async-start | bytes 131072 | tf_op jit(solution)/shard_map/all_to_all | solution.py:351
  32.0 0.3 collective-permute-start.3
  32.3 1.7 %shard_map.125 = (f32[88,512]{1,0:T(8,128)S(1)}, f32[16,512]{1,0:T(8,128)S(1)}) custom-call(s32[1]{0:T(128)} %bitcast.me_ref, f32[80,512]{1,0:T(8,128)S(1)} %get-tuple-element.24.own_ref, f32[96,512]{1,0:T(8,128)S(1)} %collective-permute-done.4.across_ref, f32[4,16,512]{2,1,0:T(8,128)S(1)} %get-tuple-element.23.part_ref), custom_call_target="tpu_custom_call" | custom-call | flops 2000000000 | tf_op jit(solution)/shard_map/pallas_call | solution.py:264
  33.9 0.0 collective-permute-done.5.corner_ref
  34.0 0.0 copy-start.6
  34.0 0.0 copy-start.7
  34.0 2.4 %shard_map.126 = (f32[81,512]{1,0:T(8,128)}, f32[27,256]{1,0:T(8,128)}) custom-call(s32[1]{0:T(128)} %bitcast.me_ref, f32[80,512]{1,0:T(8,128)S(1)} %collective-permute-done.3.beside_ref, f32[96,512]{1,0:T(8,128)S(1)} %collective-permute-done.5.corner_ref, f32[88,512]{1,0:T(8,128)S(1)} %get-tuple-element.26.total_ref, f32[16,512]{1,0:T(8,128)S(1)} %get-tuple-element.27.part_ref), custom_call_target="tpu_custom_call" | custom-call | flops 2000000000 | tf_op jit(solution)/shard_map/pallas_call | solution.py:264
  36.3 2.5 %all-to-all-done.1.back_ref = f32[8,4,512]{2,1,0:T(4,128)S(1)} async-done(((f32[8,4,512]{2,1,0:T(4,128)}), f32[8,4,512]{2,1,0:T(4,128)S(1)}, u32[]{:S(2)}, u32[]{:S(2)}) %all-to-all-start.1) | async-done | bytes 65568 | tf_op jit(solution)/shard_map/all_to_all | solution.py:351
  38.9 1.0 %shard_map.127 = f32[3,2048]{1,0:T(4,128)} custom-call(f32[8,4,512]{2,1,0:T(4,128)S(1)} %all-to-all-done.1.back_ref, s32[1,2048]{1,0:T(1,128)S(1)} %bitcast.8, s32[1,2048]{1,0:T(1,128)S(1)} %copy-done.7, f32[3,2048]{1,0:T(4,128)S(1)} %get-tuple-element.33.push_ref), custom_call_target="tpu_custom_call" | custom-call | flops 100000000 | tf_op jit(solution)/shard_map/pallas_call | solution.py:264
  (15 shorter events, 0.0 us)
Async XLA Ops:
  0.6 2.2 %copy-start.2 = (f32[27,256]{1,0:T(8,128)S(1)}, f32[27,256]{1,0:T(8,128)}, u32[]{:S(2)}) copy-start(f32[27,256]{1,0:T(8,128)} %refs_0_) | copy-start | bytes 82948
  0.6 12.6 %copy-start.1 = (f32[81,2048]{1,0:T(8,128)S(1)}, f32[81,2048]{1,0:T(8,128)}, u32[]{:S(2)}) copy-start(f32[81,2048]{1,0:T(8,128)} %refs_7_.1) | copy-start | bytes 1990660
  2.9 9.0 %collective-permute-start.1 = (f32[27,256]{1,0:T(8,128)S(1)}, f32[27,256]{1,0:T(8,128)S(1)}, u32[]{:S(2)}, u32[]{:S(2)}) collective-permute-start(f32[27,256]{1,0:T(8,128)S(1)} %copy-done.2), channel_id=1, source_target_pairs={{0,2},{1,3},{2,0},{3,1},{4,6},{5,7},{6,4},{7,5},{8,10},{9,11},{10,... | collective-permute-start | bytes 82952 | tf_op jit(solution)/shard_map/ppermute | solution.py:294
  5.9 7.4 %copy-start.4 = (f32[2,2048]{1,0:T(2,128)S(1)}, f32[2,2048]{1,0:T(2,128)}, u32[]{:S(2)}) copy-start(f32[2,2048]{1,0:T(2,128)} %refs_5_.1) | copy-start | bytes 49156
  5.9 7.4 %copy-start.5 = (s32[2048]{0:T(1024)S(1)}, s32[2048]{0:T(1024)}, u32[]{:S(2)}) copy-start(s32[2048]{0:T(1024)} %param.17) | copy-start | bytes 24580
  5.9 13.3 %all-to-all-start = ((f32[8,8,512]{2,1,0:T(8,128)}), f32[8,8,512]{2,1,0:T(8,128)S(1)}, u32[]{:S(2)}, u32[]{:S(2)}) async-start(f32[8,8,512]{2,1,0:T(8,128)} %get-tuple-element.20.sent_ref), calls=%async_computation | async-start | bytes 262144 | tf_op jit(solution)/shard_map/all_to_all | solution.py:317
  11.8 1.5 %copy-start.3 = (f32[3,2048]{1,0:T(4,128)S(1)}, f32[3,2048]{1,0:T(4,128)}, u32[]{:S(2)}) copy-start(f32[3,2048]{1,0:T(4,128)} %refs_6_.1) | copy-start | bytes 73732
  11.8 1.3 %collective-permute-start = (f32[27,256]{1,0:T(8,128)S(1)}, f32[27,256]{1,0:T(8,128)S(1)}, u32[]{:S(2)}, u32[]{:S(2)}) collective-permute-start(f32[27,256]{1,0:T(8,128)S(1)} %copy-done.2), channel_id=1, source_target_pairs={{0,1},{1,0},{2,3},{3,2},{4,5},{5,4},{6,7},{7,6},{8,9},{9,8},{10,11... | collective-permute-start | bytes 82952 | tf_op jit(solution)/shard_map/ppermute | solution.py:294
  11.9 1.4 %collective-permute-start.2 = (f32[27,256]{1,0:T(8,128)S(1)}, f32[27,256]{1,0:T(8,128)S(1)}, u32[]{:S(2)}, u32[]{:S(2)}) collective-permute-start(f32[27,256]{1,0:T(8,128)S(1)} %collective-permute-done.1.refs_2_), channel_id=1, source_target_pairs={{0,1},{1,0},{2,3},{3,2},{4,5},{5,4},{6,7},{7,6},{8,9},{9,8},{10,11... | collective-permute-start | bytes 82952 | tf_op jit(solution)/shard_map/ppermute | solution.py:294
  13.3 1.5 %copy-start = (f32[8,8,512]{2,1,0:T(8,128)S(1)}, f32[8,8,512]{2,1,0:T(8,128)}, u32[]{:S(2)}) copy-start(f32[8,8,512]{2,1,0:T(8,128)} %get-tuple-element.20.sent_ref) | copy-start | bytes 393220
  22.7 5.7 %collective-permute-start.4 = (f32[96,512]{1,0:T(8,128)S(1)}, f32[96,512]{1,0:T(8,128)S(1)}, u32[]{:S(2)}, u32[]{:S(2)}) collective-permute-start(f32[96,512]{1,0:T(8,128)S(1)} %get-tuple-element.25), channel_id=1, source_target_pairs={{0,2},{1,3},{2,0},{3,1},{4,6},{5,7},{6,4},{7,5},{8,10},{9,11},{10,... | collective-permute-start | bytes 589832 | tf_op jit(solution)/shard_map/ppermute | solution.py:294
  28.3 5.6 %collective-permute-start.5 = (f32[96,512]{1,0:T(8,128)S(1)}, f32[96,512]{1,0:T(8,128)S(1)}, u32[]{:S(2)}, u32[]{:S(2)}) collective-permute-start(f32[96,512]{1,0:T(8,128)S(1)} %collective-permute-done.4.across_ref), channel_id=1, source_target_pairs={{0,1},{1,0},{2,3},{3,2},{4,5},{5,4},{6,7},{7,6},{8,9},{9,8},{10,11... | collective-permute-start | bytes 589832 | tf_op jit(solution)/shard_map/ppermute | solution.py:294
  28.3 10.5 %all-to-all-start.1 = ((f32[8,4,512]{2,1,0:T(4,128)}), f32[8,4,512]{2,1,0:T(4,128)S(1)}, u32[]{:S(2)}, u32[]{:S(2)}) async-start(f32[8,4,512]{2,1,0:T(4,128)} %get-tuple-element.31), calls=%async_computation.1 | async-start | bytes 131072 | tf_op jit(solution)/shard_map/all_to_all | solution.py:351
  32.0 2.0 %collective-permute-start.3 = (f32[80,512]{1,0:T(8,128)S(1)}, f32[80,512]{1,0:T(8,128)S(1)}, u32[]{:S(2)}, u32[]{:S(2)}) collective-permute-start(f32[80,512]{1,0:T(8,128)S(1)} %get-tuple-element.24.own_ref), channel_id=1, source_target_pairs={{0,1},{1,0},{2,3},{3,2},{4,5},{5,4},{6,7},{7,6},{8,9},{9,8},{10,11... | collective-permute-start | bytes 491528 | tf_op jit(solution)/shard_map/ppermute | solution.py:294
  34.0 4.9 %copy-start.6 = (s32[2048,1]{0,1:T(1,128)S(1)}, s32[2048,1]{0,1:T(1,128)}, u32[]{:S(2)}) copy-start(s32[2048,1]{0,1:T(1,128)} %param.11) | copy-start | bytes 24580
  34.0 4.9 %copy-start.7 = (s32[1,2048]{1,0:T(1,128)S(1)}, s32[1,2048]{1,0:T(1,128)}, u32[]{:S(2)}) copy-start(s32[1,2048]{1,0:T(1,128)} %get-tuple-element.32.rank_ref) | copy-start | bytes 24580

commit v4 on v3

--- a/solution.py
+++ b/solution.py
@@ -108,8 +108,9 @@
 
 def contact_kernel(me_ref, *refs, peers):
     ctrl_refs = refs[:peers]
-    patch_ref, param_ref, pos_ref, coef_ref = refs[peers : peers + 4]
-    push_ref, part_ref, table_ref, ctrl, tight, wide = refs[peers + 4 :]
+    patch_ref, param_ref, pos_ref, coef_ref, rank_ref = refs[peers : peers + 5]
+    push_ref, part_ref, table_ref, place_ref, ctrl, tight, wide = refs[peers + 5 :]
+    place_ref[...] = one_hot(rank_ref[...], place_ref.shape[0])
     own = ctrl_refs[0].shape[1]
     me = me_ref[0]
     ctrl[...] = jnp.zeros_like(ctrl)
@@ -242,11 +243,11 @@
     patch_ref[14:27] = part[0:13, own:]
 
 
-def finish_kernel(back_ref, block_ref, rank_ref, push_ref, out_ref, rows):
-    owners, _, slots = back_ref.shape
+def finish_kernel(back_ref, block_ref, place_ref, push_ref, out_ref, rows):
+    owners = back_ref.shape[0]
     for d in range(owners):
         rows[d * 4 : (d + 1) * 4] = back_ref[d]
-    got = dot(split(rows[...]), one_hot(rank_ref[...], slots), NN)
+    got = dot(split(rows[...]), place_ref[...], NN)
     got = got[: owners * 4] + got[owners * 4 :]
     block = block_ref[...]
     half = rows_of((8, 1)) // 4
@@ -318,16 +319,19 @@
     twin = swap(here, 1)
     diag = swap(far, 1)
     ctrl = (here, twin, far, diag)
-    pushes, part, table = call(
+    pushes, part, table, place = call(
         functools.partial(contact_kernel, peers=peers),
-        [shape(3, count), shape(peers, 16, 2 * own), shape(176, elements, dtype=BF16)],
+        [
+            shape(3, count), shape(peers, 16, 2 * own), shape(176, elements, dtype=BF16),
+            shape(slots, count, dtype=F8),
+        ],
         scratch=[
             pltpu.VMEM((48, peers * own), F32),
             pltpu.VMEM((32, peers * own), F32),
             pltpu.VMEM((88, elements), F32),
         ],
         smem=1,
-        operands=(me, *ctrl, contact_patch.reshape(1, count), contact_param, gp_pos, vel_coef),
+        operands=(me, *ctrl, contact_patch.reshape(1, count), contact_param, gp_pos, vel_coef, rank),
         flops=10**9,
     )
     tail = groups * 8
@@ -372,7 +376,7 @@
     shell_force = call(
         finish_kernel, shape(3, count),
         scratch=[pltpu.VMEM((owners * 4, slots), F32)],
-        operands=(back, block, rank, pushes),
+        operands=(back, block, place, pushes),
         flops=10**8,
     )
     return flow_force, shell_force, patch_force

time: 40.2 us -> 40.4 us (level)
  transfers between devices with their start and end apart: 8 -> 8, of which waited for: 5 -> 5; matrix products, arithmetic and copies ran while one was open for 0% -> 0% of each run, Pallas kernels for 15% -> 16%
where the time goes in v4:
time: 40.4 us; the launch traced here: 40 us
  starting transfers between devices  14.1 us (35%)
  Pallas kernels  12.9 us (32%)
  waiting for transfers between devices  12.2 us (30%)
  between operations  0.75 us (2%)
    pallas_call x7, Pallas kernels, call(): pl.pallas_call(kernel, out_shape=out_shape, in_specs=specs, out_specs=jax...  12.9 us
    ppermute x6, waiting for transfers between devices, swap(): return lax.ppermute(x, 'leaf', [(i, i ^ k) for i in range(peers)])  6.03 us
    all_to_all x1, starting transfers between devices, per_device(): lax.all_to_all(payload, 'flow', split_axis=0, concat_axis=0, tiled=True)  5.94 us
    ppermute x6, starting transfers between devices, swap(): return lax.ppermute(x, 'leaf', [(i, i ^ k) for i in range(peers)])  4.29 us
    all_to_all x1, starting transfers between devices, per_device(): lax.all_to_all(to_owners(force), 'flow', split_axis=0, concat_axis=0, til...  3.83 us
    all_to_all x1, waiting for transfers between devices, per_device(): lax.all_to_all(payload, 'flow', split_axis=0, concat_axis=0, tiled=True)  3.6 us
    all_to_all x1, waiting for transfers between devices, per_device(): lax.all_to_all(to_owners(force), 'flow', split_axis=0, concat_axis=0, til...  2.62 us
  transfers between devices with their start and end apart: 8, of which 5 were waited for; matrix products, arithmetic and copies ran while one was open for 0% of the time, Pallas kernels for 16%

profile of v4, /device:TPU:0, one launch (start us, length us, event | category | flops | bytes accessed | tf_op | source)
XLA Modules:
  0.0 40.0 jit_solution(13872145900072855507)
XLA Ops:
  0.7 2.2 %shard_map.121 = (f32[8,8,512]{2,1,0:T(8,128)}, s32[1,2048]{1,0:T(1,128)}) custom-call(s32[1,2048]{1,0:T(1,128)} %bitcast.6, s32[1,2048]{1,0:T(1,128)} %bitcast.9, f32[3,2048]{1,0:T(4,128)} %param_ref.1, f32[3,2048]{1,0:T(4,128)} %vel_ref.1, f32[1,2048]{1,0:T(1,128)} %bitcast.10), custom_call_target="tpu_custom_call" | custom-call | flops 1000000000 | tf_op jit(solution)/shard_map/pallas_call | solution.py:265
  2.9 3.0 %collective-permute-start.1 = (f32[27,256]{1,0:T(8,128)S(1)}, f32[27,256]{1,0:T(8,128)S(1)}, u32[]{:S(2)}, u32[]{:S(2)}) collective-permute-start(f32[27,256]{1,0:T(8,128)S(1)} %copy-done.3), channel_id=1, source_target_pairs={{0,2},{1,3},{2,0},{3,1},{4,6},{5,7},{6,4},{7,5},{8,10},{9,11},{10,... | collective-permute-start | bytes 82952 | tf_op jit(solution)/shard_map/ppermute | solution.py:295
  5.9 5.9 %all-to-all-start = ((f32[8,8,512]{2,1,0:T(8,128)}), f32[8,8,512]{2,1,0:T(8,128)S(1)}, u32[]{:S(2)}, u32[]{:S(2)}) async-start(f32[8,8,512]{2,1,0:T(8,128)} %get-tuple-element.21.sent_ref), calls=%async_computation | async-start | bytes 262144 | tf_op jit(solution)/shard_map/all_to_all | solution.py:318
  11.8 0.1 collective-permute-start
  11.9 0.5 %collective-permute-start.2 = (f32[27,256]{1,0:T(8,128)S(1)}, f32[27,256]{1,0:T(8,128)S(1)}, u32[]{:S(2)}, u32[]{:S(2)}) collective-permute-start(f32[27,256]{1,0:T(8,128)S(1)} %collective-permute-done.1.refs_2_), channel_id=1, source_target_pairs={{0,1},{1,0},{2,3},{3,2},{4,5},{5,4},{6,7},{7,6},{8,9},{9,8},{10,11... | collective-permute-start | bytes 82952 | tf_op jit(solution)/shard_map/ppermute | solution.py:295
  12.4 0.7 %collective-permute-done.refs_1_ = f32[27,256]{1,0:T(8,128)S(1)} collective-permute-done((f32[27,256]{1,0:T(8,128)S(1)}, f32[27,256]{1,0:T(8,128)S(1)}, u32[]{:S(2)}, u32[]{:S(2)}) %collective-permute-start) | collective-permute-done | bytes 27680 | tf_op jit(solution)/shard_map/ppermute | solution.py:295
  13.1 0.2 collective-permute-done.2.refs_3_
  13.3 0.0 copy-start
  13.3 1.7 %shard_map.122 = (f32[3,2048]{1,0:T(4,128)S(1)}, f32[4,16,512]{2,1,0:T(8,128)S(1)}, bf16[176,2048]{1,0:T(8,128)(2,1)S(1)}, f8e4m3fn[512,2048]{1,0:T(32,128)(4,1)S(1)}) custom-call(s32[1]{0:T(128)} %bitcast.me_ref, f32[27,256]{1,0:T(8,128)S(1)} %copy-done.3, f32[27,256]{1,0:T(8,128)S(1)} %collective-permute-done.refs_1_, ...), custom_call_target="tpu_custom_call" | custom-call | flops 1000000000 | tf_op jit(solution)/shard_map/pallas_call | solution.py:265
  15.0 0.6 %shard_map.123.refs_0_ = f32[8,512]{1,0:T(8,128)S(1)} custom-call(s32[1]{0:T(128)S(6)} %select_n.7.row_ref, f32[8,8,512]{2,1,0:T(8,128)S(1)} %copy-done, bf16[176,2048]{1,0:T(8,128)(2,1)S(1)} %get-tuple-element.24.table_ref), custom_call_target="tpu_custom_call" | custom-call | flops 1000000000 | tf_op jit(solution)/shard_map/pallas_call | solution.py:265
  15.5 3.6 %all-to-all-done.recv_ref = f32[8,8,512]{2,1,0:T(8,128)S(1)} async-done(((f32[8,8,512]{2,1,0:T(8,128)}), f32[8,8,512]{2,1,0:T(8,128)S(1)}, u32[]{:S(2)}, u32[]{:S(2)}) %all-to-all-start) | async-done | bytes 131104 | tf_op jit(solution)/shard_map/all_to_all | solution.py:318
  19.1 3.5 %shard_map.124 = (f32[8,4,512]{2,1,0:T(4,128)}, f32[80,512]{1,0:T(8,128)S(1)}, f32[96,512]{1,0:T(8,128)S(1)}) custom-call(s32[1]{0:T(128)S(6)} %select_n.7.row_ref, f32[8,8,512]{2,1,0:T(8,128)S(1)} %all-to-all-done.recv_ref, bf16[176,2048]{1,0:T(8,128)(2,1)S(1)} %get-tuple-element.24.table_ref, f32[4,16,512]{2,1,0:T(8,128)S(1)} %get-tuple-element.25.part_ref, ...), custom_call_target="tpu_custom_call" | custom-call | flops 4000000000 | tf_op jit(solution)/shard_map/pallas_call | solution.py:265
  22.7 0.5 %collective-permute-start.4 = (f32[96,512]{1,0:T(8,128)S(1)}, f32[96,512]{1,0:T(8,128)S(1)}, u32[]{:S(2)}, u32[]{:S(2)}) collective-permute-start(f32[96,512]{1,0:T(8,128)S(1)} %get-tuple-element.27), channel_id=1, source_target_pairs={{0,2},{1,3},{2,0},{3,1},{4,6},{5,7},{6,4},{7,5},{8,10},{9,11},{10,... | collective-permute-start | bytes 589832 | tf_op jit(solution)/shard_map/ppermute | solution.py:295
  23.2 5.2 %collective-permute-done.4.across_ref = f32[96,512]{1,0:T(8,128)S(1)} collective-permute-done((f32[96,512]{1,0:T(8,128)S(1)}, f32[96,512]{1,0:T(8,128)S(1)}, u32[]{:S(2)}, u32[]{:S(2)}) %collective-permute-start.4) | collective-permute-done | bytes 196640 | tf_op jit(solution)/shard_map/ppermute | solution.py:295
  28.3 0.0 collective-permute-start.5
  28.3 3.8 %all-to-all-start.1 = ((f32[8,4,512]{2,1,0:T(4,128)}), f32[8,4,512]{2,1,0:T(4,128)S(1)}, u32[]{:S(2)}, u32[]{:S(2)}) async-start(f32[8,4,512]{2,1,0:T(4,128)} %get-tuple-element.33), calls=%async_computation.1 | async-start | bytes 131072 | tf_op jit(solution)/shard_map/all_to_all | solution.py:355
  32.2 0.2 collective-permute-start.3
  32.4 1.7 %shard_map.125 = (f32[88,512]{1,0:T(8,128)S(1)}, f32[16,512]{1,0:T(8,128)S(1)}) custom-call(s32[1]{0:T(128)} %bitcast.me_ref, f32[80,512]{1,0:T(8,128)S(1)} %get-tuple-element.26.own_ref, f32[96,512]{1,0:T(8,128)S(1)} %collective-permute-done.4.across_ref, f32[4,16,512]{2,1,0:T(8,128)S(1)} %get-tuple-element.25.part_ref), custom_call_target="tpu_custom_call" | custom-call | flops 2000000000 | tf_op jit(solution)/shard_map/pallas_call | solution.py:265
  34.1 0.0 collective-permute-done.3.beside_ref
  34.1 0.0 collective-permute-done.5.corner_ref
  34.1 0.0 copy-start.1
  34.1 2.4 %shard_map.126 = (f32[81,512]{1,0:T(8,128)}, f32[27,256]{1,0:T(8,128)}) custom-call(s32[1]{0:T(128)} %bitcast.me_ref, f32[80,512]{1,0:T(8,128)S(1)} %collective-permute-done.3.beside_ref, f32[96,512]{1,0:T(8,128)S(1)} %collective-permute-done.5.corner_ref, f32[88,512]{1,0:T(8,128)S(1)} %get-tuple-element.28.total_ref, f32[16,512]{1,0:T(8,128)S(1)} %get-tuple-element.29.part_ref), custom_call_target="tpu_custom_call" | custom-call | flops 2000000000 | tf_op jit(solution)/shard_map/pallas_call | solution.py:265
  36.4 2.6 %all-to-all-done.1.back_ref = f32[8,4,512]{2,1,0:T(4,128)S(1)} async-done(((f32[8,4,512]{2,1,0:T(4,128)}), f32[8,4,512]{2,1,0:T(4,128)S(1)}, u32[]{:S(2)}, u32[]{:S(2)}) %all-to-all-start.1) | async-done | bytes 65568 | tf_op jit(solution)/shard_map/all_to_all | solution.py:355
  39.1 0.9 %shard_map.127 = f32[3,2048]{1,0:T(4,128)} custom-call(f32[8,4,512]{2,1,0:T(4,128)S(1)} %all-to-all-done.1.back_ref, s32[1,2048]{1,0:T(1,128)S(1)} %bitcast.7, f8e4m3fn[512,2048]{1,0:T(32,128)(4,1)S(1)} %get-tuple-element.34.place_ref, f32[3,2048]{1,0:T(4,128)S(1)} %get-tuple-element.35.push_ref), custom_call_target="tpu_custom_call" | custom-call | flops 100000000 | tf_op jit(solution)/shard_map/pallas_call | solution.py:265
  (15 shorter events, 0.0 us)
Async XLA Ops:
  0.6 2.2 %copy-start.3 = (f32[27,256]{1,0:T(8,128)S(1)}, f32[27,256]{1,0:T(8,128)}, u32[]{:S(2)}) copy-start(f32[27,256]{1,0:T(8,128)} %refs_0_) | copy-start | bytes 82948
  0.6 12.6 %copy-start.2 = (f32[81,2048]{1,0:T(8,128)S(1)}, f32[81,2048]{1,0:T(8,128)}, u32[]{:S(2)}) copy-start(f32[81,2048]{1,0:T(8,128)} %refs_7_.1) | copy-start | bytes 1990660
  2.9 9.0 %collective-permute-start.1 = (f32[27,256]{1,0:T(8,128)S(1)}, f32[27,256]{1,0:T(8,128)S(1)}, u32[]{:S(2)}, u32[]{:S(2)}) collective-permute-start(f32[27,256]{1,0:T(8,128)S(1)} %copy-done.3), channel_id=1, source_target_pairs={{0,2},{1,3},{2,0},{3,1},{4,6},{5,7},{6,4},{7,5},{8,10},{9,11},{10,... | collective-permute-start | bytes 82952 | tf_op jit(solution)/shard_map/ppermute | solution.py:295
  5.9 7.4 %copy-start.5 = (f32[2,2048]{1,0:T(2,128)S(1)}, f32[2,2048]{1,0:T(2,128)}, u32[]{:S(2)}) copy-start(f32[2,2048]{1,0:T(2,128)} %refs_5_.1) | copy-start | bytes 49156
  5.9 7.4 %copy-start.7 = (s32[1,2048]{1,0:T(1,128)S(1)}, s32[1,2048]{1,0:T(1,128)}, u32[]{:S(2)}) copy-start(s32[1,2048]{1,0:T(1,128)} %get-tuple-element.23.refs_8_) | copy-start | bytes 24580
  5.9 13.3 %all-to-all-start = ((f32[8,8,512]{2,1,0:T(8,128)}), f32[8,8,512]{2,1,0:T(8,128)S(1)}, u32[]{:S(2)}, u32[]{:S(2)}) async-start(f32[8,8,512]{2,1,0:T(8,128)} %get-tuple-element.21.sent_ref), calls=%async_computation | async-start | bytes 262144 | tf_op jit(solution)/shard_map/all_to_all | solution.py:318
  11.8 1.5 %copy-start.4 = (f32[3,2048]{1,0:T(4,128)S(1)}, f32[3,2048]{1,0:T(4,128)}, u32[]{:S(2)}) copy-start(f32[3,2048]{1,0:T(4,128)} %refs_6_.1) | copy-start | bytes 73732
  11.8 1.3 %collective-permute-start = (f32[27,256]{1,0:T(8,128)S(1)}, f32[27,256]{1,0:T(8,128)S(1)}, u32[]{:S(2)}, u32[]{:S(2)}) collective-permute-start(f32[27,256]{1,0:T(8,128)S(1)} %copy-done.3), channel_id=1, source_target_pairs={{0,1},{1,0},{2,3},{3,2},{4,5},{5,4},{6,7},{7,6},{8,9},{9,8},{10,11... | collective-permute-start | bytes 82952 | tf_op jit(solution)/shard_map/ppermute | solution.py:295
  11.9 1.4 %collective-permute-start.2 = (f32[27,256]{1,0:T(8,128)S(1)}, f32[27,256]{1,0:T(8,128)S(1)}, u32[]{:S(2)}, u32[]{:S(2)}) collective-permute-start(f32[27,256]{1,0:T(8,128)S(1)} %collective-permute-done.1.refs_2_), channel_id=1, source_target_pairs={{0,1},{1,0},{2,3},{3,2},{4,5},{5,4},{6,7},{7,6},{8,9},{9,8},{10,11... | collective-permute-start | bytes 82952 | tf_op jit(solution)/shard_map/ppermute | solution.py:295
  12.4 0.9 %copy-start.6 = (s32[2048]{0:T(1024)S(1)}, s32[2048]{0:T(1024)}, u32[]{:S(2)}) copy-start(s32[2048]{0:T(1024)} %param.17) | copy-start | bytes 24580
  13.3 1.7 %copy-start = (f32[8,8,512]{2,1,0:T(8,128)S(1)}, f32[8,8,512]{2,1,0:T(8,128)}, u32[]{:S(2)}) copy-start(f32[8,8,512]{2,1,0:T(8,128)} %get-tuple-element.21.sent_ref) | copy-start | bytes 393220
  22.7 5.7 %collective-permute-start.4 = (f32[96,512]{1,0:T(8,128)S(1)}, f32[96,512]{1,0:T(8,128)S(1)}, u32[]{:S(2)}, u32[]{:S(2)}) collective-permute-start(f32[96,512]{1,0:T(8,128)S(1)} %get-tuple-element.27), channel_id=1, source_target_pairs={{0,2},{1,3},{2,0},{3,1},{4,6},{5,7},{6,4},{7,5},{8,10},{9,11},{10,... | collective-permute-start | bytes 589832 | tf_op jit(solution)/shard_map/ppermute | solution.py:295
  28.3 5.7 %collective-permute-start.5 = (f32[96,512]{1,0:T(8,128)S(1)}, f32[96,512]{1,0:T(8,128)S(1)}, u32[]{:S(2)}, u32[]{:S(2)}) collective-permute-start(f32[96,512]{1,0:T(8,128)S(1)} %collective-permute-done.4.across_ref), channel_id=1, source_target_pairs={{0,1},{1,0},{2,3},{3,2},{4,5},{5,4},{6,7},{7,6},{8,9},{9,8},{10,11... | collective-permute-start | bytes 589832 | tf_op jit(solution)/shard_map/ppermute | solution.py:295
  28.3 10.7 %all-to-all-start.1 = ((f32[8,4,512]{2,1,0:T(4,128)}), f32[8,4,512]{2,1,0:T(4,128)S(1)}, u32[]{:S(2)}, u32[]{:S(2)}) async-start(f32[8,4,512]{2,1,0:T(4,128)} %get-tuple-element.33), calls=%async_computation.1 | async-start | bytes 131072 | tf_op jit(solution)/shard_map/all_to_all | solution.py:355
  32.2 1.9 %collective-permute-start.3 = (f32[80,512]{1,0:T(8,128)S(1)}, f32[80,512]{1,0:T(8,128)S(1)}, u32[]{:S(2)}, u32[]{:S(2)}) collective-permute-start(f32[80,512]{1,0:T(8,128)S(1)} %get-tuple-element.26.own_ref), channel_id=1, source_target_pairs={{0,1},{1,0},{2,3},{3,2},{4,5},{5,4},{6,7},{7,6},{8,9},{9,8},{10,11... | collective-permute-start | bytes 491528 | tf_op jit(solution)/shard_map/ppermute | solution.py:295
  34.1 5.0 %copy-start.1 = (s32[2048,1]{0,1:T(1,128)S(1)}, s32[2048,1]{0,1:T(1,128)}, u32[]{:S(2)}) copy-start(s32[2048,1]{0,1:T(1,128)} %param.11) | copy-start | bytes 24580

commit v5 on v4

--- a/solution.py
+++ b/solution.py
@@ -11,6 +11,7 @@
 BETA = 1.5
 STIFF = 2.0
 REACH = 0.5
+BATCH = 2
 VMEM_LIMIT = 20 * 2**20
 GROUP = 512
 
@@ -183,13 +184,17 @@
         back_ref[g] = both[4:8]
 
     first = row_ref[0]
-    for r in range(groups):
-        g = lax.rem(first + r, groups)
-        point = recv_ref[g]
-        if homes and r == 0:
-            put(g, point, [homes[0][c : c + 1] for c in range(3)])
-        else:
-            put(g, point, force_of(point, table_ref))
+    order = [lax.rem(first + r, groups) for r in range(groups)]
+    if homes:
+        put(order[0], recv_ref[order[0]], [homes[0][c : c + 1] for c in range(3)])
+        order = order[1:]
+    for i in range(0, len(order), BATCH):
+        batch = order[i : i + BATCH]
+        point = jnp.concatenate([recv_ref[g] for g in batch], axis=1)
+        forces = force_of(point, table_ref)
+        for j, g in enumerate(batch):
+            here = slice(j * GROUP, (j + 1) * GROUP)
+            put(g, point[:, here], [f[:, here] for f in forces])
     tail = groups * 8
     beside_ref[tail:] = part_ref[1]
     across_ref[tail : tail + 16] = part_ref[2]

time: 40.4 us -> 40.4 us (level)
  no operation moved by 1% of the time
where the time goes in v5:
time: 40.4 us; the launch traced here: 40 us
  starting transfers between devices  14.1 us (35%)
  Pallas kernels  12.9 us (32%)
  waiting for transfers between devices  12.2 us (30%)
  between operations  0.75 us (2%)
    pallas_call x7, Pallas kernels, call(): pl.pallas_call(kernel, out_shape=out_shape, in_specs=specs, out_specs=jax...  12.9 us
    ppermute x6, waiting for transfers between devices, swap(): return lax.ppermute(x, 'leaf', [(i, i ^ k) for i in range(peers)])  6.03 us
    all_to_all x1, starting transfers between devices, per_device(): lax.all_to_all(payload, 'flow', split_axis=0, concat_axis=0, tiled=True)  5.94 us
    ppermute x6, starting transfers between devices, swap(): return lax.ppermute(x, 'leaf', [(i, i ^ k) for i in range(peers)])  4.29 us
    all_to_all x1, starting transfers between devices, per_device(): lax.all_to_all(to_owners(force), 'flow', split_axis=0, concat_axis=0, til...  3.83 us
    all_to_all x1, waiting for transfers between devices, per_device(): lax.all_to_all(payload, 'flow', split_axis=0, concat_axis=0, tiled=True)  3.6 us
    all_to_all x1, waiting for transfers between devices, per_device(): lax.all_to_all(to_owners(force), 'flow', split_axis=0, concat_axis=0, til...  2.62 us
  transfers between devices with their start and end apart: 8, of which 5 were waited for; matrix products, arithmetic and copies ran while one was open for 0% of the time, Pallas kernels for 16%

profile of v5, /device:TPU:0, one launch (start us, length us, event | category | flops | bytes accessed | tf_op | source)
XLA Modules:
  0.0 40.0 jit_solution(17471095492470575352)
XLA Ops:
  0.7 2.2 %shard_map.121 = (f32[8,8,512]{2,1,0:T(8,128)}, s32[1,2048]{1,0:T(1,128)}) custom-call(s32[1,2048]{1,0:T(1,128)} %bitcast.6, s32[1,2048]{1,0:T(1,128)} %bitcast.9, f32[3,2048]{1,0:T(4,128)} %param_ref.1, f32[3,2048]{1,0:T(4,128)} %vel_ref.1, f32[1,2048]{1,0:T(1,128)} %bitcast.10), custom_call_target="tpu_custom_call" | custom-call | flops 1000000000 | tf_op jit(solution)/shard_map/pallas_call | solution.py:270
  2.9 3.0 %collective-permute-start.1 = (f32[27,256]{1,0:T(8,128)S(1)}, f32[27,256]{1,0:T(8,128)S(1)}, u32[]{:S(2)}, u32[]{:S(2)}) collective-permute-start(f32[27,256]{1,0:T(8,128)S(1)} %copy-done.3), channel_id=1, source_target_pairs={{0,2},{1,3},{2,0},{3,1},{4,6},{5,7},{6,4},{7,5},{8,10},{9,11},{10,... | collective-permute-start | bytes 82952 | tf_op jit(solution)/shard_map/ppermute | solution.py:300
  5.9 5.9 %all-to-all-start = ((f32[8,8,512]{2,1,0:T(8,128)}), f32[8,8,512]{2,1,0:T(8,128)S(1)}, u32[]{:S(2)}, u32[]{:S(2)}) async-start(f32[8,8,512]{2,1,0:T(8,128)} %get-tuple-element.21.sent_ref), calls=%async_computation | async-start | bytes 262144 | tf_op jit(solution)/shard_map/all_to_all | solution.py:323
  11.8 0.1 collective-permute-start
  11.9 0.0 collective-permute-done.1.refs_2_
  11.9 0.5 %collective-permute-start.2 = (f32[27,256]{1,0:T(8,128)S(1)}, f32[27,256]{1,0:T(8,128)S(1)}, u32[]{:S(2)}, u32[]{:S(2)}) collective-permute-start(f32[27,256]{1,0:T(8,128)S(1)} %collective-permute-done.1.refs_2_), channel_id=1, source_target_pairs={{0,1},{1,0},{2,3},{3,2},{4,5},{5,4},{6,7},{7,6},{8,9},{9,8},{10,11... | collective-permute-start | bytes 82952 | tf_op jit(solution)/shard_map/ppermute | solution.py:300
  12.4 0.7 %collective-permute-done.refs_1_ = f32[27,256]{1,0:T(8,128)S(1)} collective-permute-done((f32[27,256]{1,0:T(8,128)S(1)}, f32[27,256]{1,0:T(8,128)S(1)}, u32[]{:S(2)}, u32[]{:S(2)}) %collective-permute-start) | collective-permute-done | bytes 27680 | tf_op jit(solution)/shard_map/ppermute | solution.py:300
  13.1 0.2 collective-permute-done.2.refs_3_
  13.3 0.0 copy-start
  13.3 1.7 %shard_map.122 = (f32[3,2048]{1,0:T(4,128)S(1)}, f32[4,16,512]{2,1,0:T(8,128)S(1)}, bf16[176,2048]{1,0:T(8,128)(2,1)S(1)}, f8e4m3fn[512,2048]{1,0:T(32,128)(4,1)S(1)}) custom-call(s32[1]{0:T(128)} %bitcast.me_ref, f32[27,256]{1,0:T(8,128)S(1)} %copy-done.3, f32[27,256]{1,0:T(8,128)S(1)} %collective-permute-done.refs_1_, ...), custom_call_target="tpu_custom_call" | custom-call | flops 1000000000 | tf_op jit(solution)/shard_map/pallas_call | solution.py:270
  15.0 0.6 %shard_map.123.refs_0_ = f32[8,512]{1,0:T(8,128)S(1)} custom-call(s32[1]{0:T(128)S(6)} %select_n.7.row_ref, f32[8,8,512]{2,1,0:T(8,128)S(1)} %copy-done, bf16[176,2048]{1,0:T(8,128)(2,1)S(1)} %get-tuple-element.24.table_ref), custom_call_target="tpu_custom_call" | custom-call | flops 1000000000 | tf_op jit(solution)/shard_map/pallas_call | solution.py:270
  15.5 3.6 %all-to-all-done.recv_ref = f32[8,8,512]{2,1,0:T(8,128)S(1)} async-done(((f32[8,8,512]{2,1,0:T(8,128)}), f32[8,8,512]{2,1,0:T(8,128)S(1)}, u32[]{:S(2)}, u32[]{:S(2)}) %all-to-all-start) | async-done | bytes 131104 | tf_op jit(solution)/shard_map/all_to_all | solution.py:323
  19.1 3.5 %shard_map.124 = (f32[8,4,512]{2,1,0:T(4,128)}, f32[80,512]{1,0:T(8,128)S(1)}, f32[96,512]{1,0:T(8,128)S(1)}) custom-call(s32[1]{0:T(128)S(6)} %select_n.7.row_ref, f32[8,8,512]{2,1,0:T(8,128)S(1)} %all-to-all-done.recv_ref, bf16[176,2048]{1,0:T(8,128)(2,1)S(1)} %get-tuple-element.24.table_ref, f32[4,16,512]{2,1,0:T(8,128)S(1)} %get-tuple-element.25.part_ref, ...), custom_call_target="tpu_custom_call" | custom-call | flops 4000000000 | tf_op jit(solution)/shard_map/pallas_call | solution.py:270
  22.7 0.5 %collective-permute-start.4 = (f32[96,512]{1,0:T(8,128)S(1)}, f32[96,512]{1,0:T(8,128)S(1)}, u32[]{:S(2)}, u32[]{:S(2)}) collective-permute-start(f32[96,512]{1,0:T(8,128)S(1)} %get-tuple-element.27), channel_id=1, source_target_pairs={{0,2},{1,3},{2,0},{3,1},{4,6},{5,7},{6,4},{7,5},{8,10},{9,11},{10,... | collective-permute-start | bytes 589832 | tf_op jit(solution)/shard_map/ppermute | solution.py:300
  23.2 5.2 %collective-permute-done.4.across_ref = f32[96,512]{1,0:T(8,128)S(1)} collective-permute-done((f32[96,512]{1,0:T(8,128)S(1)}, f32[96,512]{1,0:T(8,128)S(1)}, u32[]{:S(2)}, u32[]{:S(2)}) %collective-permute-start.4) | collective-permute-done | bytes 196640 | tf_op jit(solution)/shard_map/ppermute | solution.py:300
  28.3 0.0 collective-permute-start.5
  28.3 3.8 %all-to-all-start.1 = ((f32[8,4,512]{2,1,0:T(4,128)}), f32[8,4,512]{2,1,0:T(4,128)S(1)}, u32[]{:S(2)}, u32[]{:S(2)}) async-start(f32[8,4,512]{2,1,0:T(4,128)} %get-tuple-element.33), calls=%async_computation.1 | async-start | bytes 131072 | tf_op jit(solution)/shard_map/all_to_all | solution.py:360
  32.2 0.2 collective-permute-start.3
  32.4 1.7 %shard_map.125 = (f32[88,512]{1,0:T(8,128)S(1)}, f32[16,512]{1,0:T(8,128)S(1)}) custom-call(s32[1]{0:T(128)} %bitcast.me_ref, f32[80,512]{1,0:T(8,128)S(1)} %get-tuple-element.26.own_ref, f32[96,512]{1,0:T(8,128)S(1)} %collective-permute-done.4.across_ref, f32[4,16,512]{2,1,0:T(8,128)S(1)} %get-tuple-element.25.part_ref), custom_call_target="tpu_custom_call" | custom-call | flops 2000000000 | tf_op jit(solution)/shard_map/pallas_call | solution.py:270
  34.1 0.0 collective-permute-done.3.beside_ref
  34.1 0.0 copy-start.1
  34.1 2.4 %shard_map.126 = (f32[81,512]{1,0:T(8,128)}, f32[27,256]{1,0:T(8,128)}) custom-call(s32[1]{0:T(128)} %bitcast.me_ref, f32[80,512]{1,0:T(8,128)S(1)} %collective-permute-done.3.beside_ref, f32[96,512]{1,0:T(8,128)S(1)} %collective-permute-done.5.corner_ref, f32[88,512]{1,0:T(8,128)S(1)} %get-tuple-element.28.total_ref, f32[16,512]{1,0:T(8,128)S(1)} %get-tuple-element.29.part_ref), custom_call_target="tpu_custom_call" | custom-call | flops 2000000000 | tf_op jit(solution)/shard_map/pallas_call | solution.py:270
  36.4 2.6 %all-to-all-done.1.back_ref = f32[8,4,512]{2,1,0:T(4,128)S(1)} async-done(((f32[8,4,512]{2,1,0:T(4,128)}), f32[8,4,512]{2,1,0:T(4,128)S(1)}, u32[]{:S(2)}, u32[]{:S(2)}) %all-to-all-start.1) | async-done | bytes 65568 | tf_op jit(solution)/shard_map/all_to_all | solution.py:360
  39.1 0.9 %shard_map.127 = f32[3,2048]{1,0:T(4,128)} custom-call(f32[8,4,512]{2,1,0:T(4,128)S(1)} %all-to-all-done.1.back_ref, s32[1,2048]{1,0:T(1,128)S(1)} %bitcast.7, f8e4m3fn[512,2048]{1,0:T(32,128)(4,1)S(1)} %get-tuple-element.34.place_ref, f32[3,2048]{1,0:T(4,128)S(1)} %get-tuple-element.35.push_ref), custom_call_target="tpu_custom_call" | custom-call | flops 100000000 | tf_op jit(solution)/shard_map/pallas_call | solution.py:270
  (15 shorter events, 0.0 us)
Async XLA Ops:
  0.6 2.2 %copy-start.3 = (f32[27,256]{1,0:T(8,128)S(1)}, f32[27,256]{1,0:T(8,128)}, u32[]{:S(2)}) copy-start(f32[27,256]{1,0:T(8,128)} %refs_0_) | copy-start | bytes 82948
  0.6 12.6 %copy-start.2 = (f32[81,2048]{1,0:T(8,128)S(1)}, f32[81,2048]{1,0:T(8,128)}, u32[]{:S(2)}) copy-start(f32[81,2048]{1,0:T(8,128)} %refs_7_.1) | copy-start | bytes 1990660
  2.9 9.0 %collective-permute-start.1 = (f32[27,256]{1,0:T(8,128)S(1)}, f32[27,256]{1,0:T(8,128)S(1)}, u32[]{:S(2)}, u32[]{:S(2)}) collective-permute-start(f32[27,256]{1,0:T(8,128)S(1)} %copy-done.3), channel_id=1, source_target_pairs={{0,2},{1,3},{2,0},{3,1},{4,6},{5,7},{6,4},{7,5},{8,10},{9,11},{10,... | collective-permute-start | bytes 82952 | tf_op jit(solution)/shard_map/ppermute | solution.py:300
  5.9 7.4 %copy-start.5 = (f32[2,2048]{1,0:T(2,128)S(1)}, f32[2,2048]{1,0:T(2,128)}, u32[]{:S(2)}) copy-start(f32[2,2048]{1,0:T(2,128)} %refs_5_.1) | copy-start | bytes 49156
  5.9 7.4 %copy-start.7 = (s32[1,2048]{1,0:T(1,128)S(1)}, s32[1,2048]{1,0:T(1,128)}, u32[]{:S(2)}) copy-start(s32[1,2048]{1,0:T(1,128)} %get-tuple-element.23.refs_8_) | copy-start | bytes 24580
  5.9 13.3 %all-to-all-start = ((f32[8,8,512]{2,1,0:T(8,128)}), f32[8,8,512]{2,1,0:T(8,128)S(1)}, u32[]{:S(2)}, u32[]{:S(2)}) async-start(f32[8,8,512]{2,1,0:T(8,128)} %get-tuple-element.21.sent_ref), calls=%async_computation | async-start | bytes 262144 | tf_op jit(solution)/shard_map/all_to_all | solution.py:323
  11.8 1.5 %copy-start.4 = (f32[3,2048]{1,0:T(4,128)S(1)}, f32[3,2048]{1,0:T(4,128)}, u32[]{:S(2)}) copy-start(f32[3,2048]{1,0:T(4,128)} %refs_6_.1) | copy-start | bytes 73732
  11.8 1.3 %collective-permute-start = (f32[27,256]{1,0:T(8,128)S(1)}, f32[27,256]{1,0:T(8,128)S(1)}, u32[]{:S(2)}, u32[]{:S(2)}) collective-permute-start(f32[27,256]{1,0:T(8,128)S(1)} %copy-done.3), channel_id=1, source_target_pairs={{0,1},{1,0},{2,3},{3,2},{4,5},{5,4},{6,7},{7,6},{8,9},{9,8},{10,11... | collective-permute-start | bytes 82952 | tf_op jit(solution)/shard_map/ppermute | solution.py:300
  11.9 1.4 %collective-permute-start.2 = (f32[27,256]{1,0:T(8,128)S(1)}, f32[27,256]{1,0:T(8,128)S(1)}, u32[]{:S(2)}, u32[]{:S(2)}) collective-permute-start(f32[27,256]{1,0:T(8,128)S(1)} %collective-permute-done.1.refs_2_), channel_id=1, source_target_pairs={{0,1},{1,0},{2,3},{3,2},{4,5},{5,4},{6,7},{7,6},{8,9},{9,8},{10,11... | collective-permute-start | bytes 82952 | tf_op jit(solution)/shard_map/ppermute | solution.py:300
  12.4 0.9 %copy-start.6 = (s32[2048]{0:T(1024)S(1)}, s32[2048]{0:T(1024)}, u32[]{:S(2)}) copy-start(s32[2048]{0:T(1024)} %param.17) | copy-start | bytes 24580
  13.3 1.7 %copy-start = (f32[8,8,512]{2,1,0:T(8,128)S(1)}, f32[8,8,512]{2,1,0:T(8,128)}, u32[]{:S(2)}) copy-start(f32[8,8,512]{2,1,0:T(8,128)} %get-tuple-element.21.sent_ref) | copy-start | bytes 393220
  22.7 5.7 %collective-permute-start.4 = (f32[96,512]{1,0:T(8,128)S(1)}, f32[96,512]{1,0:T(8,128)S(1)}, u32[]{:S(2)}, u32[]{:S(2)}) collective-permute-start(f32[96,512]{1,0:T(8,128)S(1)} %get-tuple-element.27), channel_id=1, source_target_pairs={{0,2},{1,3},{2,0},{3,1},{4,6},{5,7},{6,4},{7,5},{8,10},{9,11},{10,... | collective-permute-start | bytes 589832 | tf_op jit(solution)/shard_map/ppermute | solution.py:300
  28.3 5.7 %collective-permute-start.5 = (f32[96,512]{1,0:T(8,128)S(1)}, f32[96,512]{1,0:T(8,128)S(1)}, u32[]{:S(2)}, u32[]{:S(2)}) collective-permute-start(f32[96,512]{1,0:T(8,128)S(1)} %collective-permute-done.4.across_ref), channel_id=1, source_target_pairs={{0,1},{1,0},{2,3},{3,2},{4,5},{5,4},{6,7},{7,6},{8,9},{9,8},{10,11... | collective-permute-start | bytes 589832 | tf_op jit(solution)/shard_map/ppermute | solution.py:300
  28.3 10.7 %all-to-all-start.1 = ((f32[8,4,512]{2,1,0:T(4,128)}), f32[8,4,512]{2,1,0:T(4,128)S(1)}, u32[]{:S(2)}, u32[]{:S(2)}) async-start(f32[8,4,512]{2,1,0:T(4,128)} %get-tuple-element.33), calls=%async_computation.1 | async-start | bytes 131072 | tf_op jit(solution)/shard_map/all_to_all | solution.py:360
  32.2 1.9 %collective-permute-start.3 = (f32[80,512]{1,0:T(8,128)S(1)}, f32[80,512]{1,0:T(8,128)S(1)}, u32[]{:S(2)}, u32[]{:S(2)}) collective-permute-start(f32[80,512]{1,0:T(8,128)S(1)} %get-tuple-element.26.own_ref), channel_id=1, source_target_pairs={{0,1},{1,0},{2,3},{3,2},{4,5},{5,4},{6,7},{7,6},{8,9},{9,8},{10,11... | collective-permute-start | bytes 491528 | tf_op jit(solution)/shard_map/ppermute | solution.py:300
  34.1 5.0 %copy-start.1 = (s32[2048,1]{0,1:T(1,128)S(1)}, s32[2048,1]{0,1:T(1,128)}, u32[]{:S(2)}) copy-start(s32[2048,1]{0,1:T(1,128)} %param.11) | copy-start | bytes 24580
